TPU v7x, 128 devices: a whole 4x4x4 slice. The times are simulated.
128 devices in a mesh: rep: 1, r: 16 (over y, z), s: 8 (over x, core).
Axes of the slice: x: 4, y: 4, z: 4, core: 2. Of those that a mesh axis runs over, the one named last changes fastest.
Arguments:
- x: bfloat16 [128, 2048, 1024], P(('rep', 'r', 's'))
- dy: bfloat16 [128, 2048, 1024], P(('rep', 'r', 's'))
- w_gate: bfloat16 [2, 1024, 3200], P(None, 's')
- w_up: bfloat16 [2, 1024, 3200], P(None, 's')
- w_down: bfloat16 [2, 3200, 1024], P(None, 's')
- m_w_gate: float32 [2, 1024, 3200], P(None, 's')
- m_w_up: float32 [2, 1024, 3200], P(None, 's')
- m_w_down: float32 [2, 3200, 1024], P(None, 's')
- v_w_gate: float32 [2, 1024, 3200], P(None, 's')
- v_w_up: float32 [2, 1024, 3200], P(None, 's')
- v_w_down: float32 [2, 3200, 1024], P(None, 's')
Outputs:
- output 1: bfloat16 [2, 1024, 3200], P('rep', 's')
- output 2: bfloat16 [2, 1024, 3200], P('rep', 's')
- output 3: bfloat16 [2, 3200, 1024], P('rep', 's')
- output 4: float32 [2, 1024, 3200], P('rep', 's')
- output 5: float32 [2, 1024, 3200], P('rep', 's')
- output 6: float32 [2, 3200, 1024], P('rep', 's')
- output 7: float32 [2, 1024, 3200], P('rep', 's')
- output 8: float32 [2, 1024, 3200], P('rep', 's')
- output 9: float32 [2, 3200, 1024], P('rep', 's')
All inputs are finite; a program needn't handle non-finite values.
Results may differ from a plain program's by a relative error of at most 0.022.
Values are sent between devices in bfloat16 or wider.
A program may use at most 1.5 GiB of HBM per device.

v0:
```python
import jax
import jax.numpy as jnp
from jax import lax
from jax.sharding import PartitionSpec as P

NAMES = ("w_gate", "w_up", "w_down")


def matmul(a, w):
    return jnp.dot(a, w, preferred_element_type=jnp.float32).astype(jnp.bfloat16)


def normed(h):
    wide = h.astype(jnp.float32)
    scale = lax.rsqrt(jnp.mean(wide**2, -1, keepdims=True) + 1e-6)
    return (wide * scale).astype(jnp.bfloat16)


def layer(h, w):
    a = normed(h)
    gate = jnp.dot(a, w["w_gate"], preferred_element_type=jnp.float32)
    up = jnp.dot(a, w["w_up"], preferred_element_type=jnp.float32)
    return h + matmul((jax.nn.silu(gate) * up).astype(jnp.bfloat16), w["w_down"])


def adamw(w, m, v, g):
    m = 0.9 * m + 0.1 * g
    v = 0.95 * v + 0.05 * g * g
    step = m * lax.rsqrt(v + 1e-8) + 0.1 * w
    return (w - 0.02 * step).astype(jnp.bfloat16), m, v


def clipped(gradients, sum_of_squares, count):
    factor = jnp.minimum(1.0, 0.5 * lax.rsqrt(sum_of_squares / count + 1e-30))
    return [g * factor for g in gradients]


def solution(mesh):
    def fetched(weights, number):
        return {name: lax.all_gather(w[number], "s", axis=0, tiled=True) for name, w in zip(NAMES, weights, strict=True)}

    def summed(term):
        return lax.psum(lax.psum_scatter(term, "s", scatter_dimension=0, tiled=True), "r")

    def step(x, dy, *arrays):
        weights, m, v = (arrays[i : i + 3] for i in (0, 3, 6))
        layers = weights[0].shape[0]
        h, kept = x[0], []
        for number in range(layers):
            kept.append(h)
            h = layer(h, fetched(weights, number))
        by_h, mine = dy[0], [None] * layers
        for number in reversed(range(layers)):
            _, back = jax.vjp(lambda w, h: layer(h, w), fetched(weights, number), kept[number])
            by_w, by_h = back(by_h)
            mine[number] = [summed(by_w[name]) for name in NAMES]
        gradients = [jnp.stack([mine[number][i] for number in range(layers)]).astype(jnp.float32) for i in range(3)]
        squares = lax.psum(sum(jnp.sum(g * g) for g in gradients), "s")
        gradients = clipped(gradients, squares, lax.psum(1, "s") * sum(g.size for g in gradients))
        new = [adamw(w.astype(jnp.float32), m, v, g) for w, m, v, g in zip(weights, m, v, gradients, strict=True)]
        return tuple(one[which] for which in range(3) for one in new)

    states, cut = P(("rep", "r", "s"), None, None), P(None, "s", None)
    return jax.shard_map(
        step,
        mesh=mesh,
        in_specs=(states, states) + (cut,) * 9,
        out_specs=(P("rep", "s", None),) * 9,
        check_vma=False,
    )
```

profile of v0, /device:TPU:1, one launch (start us, length us, event | category | flops | bytes accessed | tf_op | source)
XLA Modules:
  0.0 823.4 jit_solution(12224919706118197217)
XLA Ops:
  7.2 2.8 fusion.94
  10.0 0.0 all-gather.15.cloned.1.call-start
  10.1 2.7 fusion.93
  12.8 0.0 all-gather.17.cloned.1.call-start
  12.8 1.3 fusion.92
  14.2 0.5 all-gather.21.cloned.1.call-update
  14.8 0.5 all-gather.23.cloned.1.call-update
  15.4 0.5 all-gather.19.cloned.1.call-update
  15.9 6.5 copy.20
  22.4 3.1 fusion.15
  25.5 6.6 copy.21
  32.1 23.5 %all-gather.13.cloned.1.call-done = bf16[1,1024,3200]{2,1,0:T(8,128)(2,1)} async-done(((bf16[1,128,3200]{2,1,0:T(8,128)(2,1)}), bf16[1,1024,3200]{2,1,0:T(8,128)(2,1)}) %all-gather.13.cloned.1.call-update) | async-done | bytes 6553616 | tf_op jit(solution)/shard_map/all_gather | solution.py:40
  55.6 22.9 %fusion.41 = f32[2048,3200]{1,0:T(8,128)} fusion(bf16[1,1024,3200]{2,1,0:T(8,128)(2,1)} %all-gather.13.cloned.1.call-done, bf16[1,2048,1024]{1,2,0:T(8,128)(2,1)} %copy.20, f32[2048]{0:T(1024)S(1)} %add_rsqrt_fusion), kind=kOutput, calls=%fused_computation.59 | convolution fusion | flops 13428064256 | bytes 36970496 | tf_op jit(solution)/shard_map/dot_general | solution.py:21
  78.5 21.3 %all-gather.15.cloned.1.call-done = bf16[1,1024,3200]{2,1,0:T(8,128)(2,1)} async-done(((bf16[1,128,3200]{2,1,0:T(8,128)(2,1)}), bf16[1,1024,3200]{2,1,0:T(8,128)(2,1)}) %all-gather.15.cloned.1.call-update) | async-done | bytes 6553616 | tf_op jit(solution)/shard_map/all_gather | solution.py:40
  99.7 31.4 %multiply_convert_fusion.1 = (bf16[2048,3200]{1,0:T(8,128)(2,1)}, f32[2048,3200]{1,0:T(8,128)}) fusion(f32[2048,3200]{1,0:T(8,128)} %fusion.41, bf16[1,1024,3200]{2,1,0:T(8,128)(2,1)} %all-gather.15.cloned.1.call-done, bf16[1,2048,1024]{1,2,0:T(8,128)(2,1)} %copy.20, f32[2048]{0:T(1024)S(1)} %add_rsqrt_fusion), kind=kOutput, calls=%fused_computation.17 | convolution fusion | flops 13467385856 | bytes 76292096 | tf_op jit(solution)/shard_map/dot_general | solution.py:22
  131.1 12.8 %all-gather.17.cloned.1.call-done = bf16[1,3200,1024]{2,1,0:T(8,128)(2,1)} async-done(((bf16[1,400,1024]{2,1,0:T(8,128)(2,1)}), bf16[1,3200,1024]{2,1,0:T(8,128)(2,1)}) %all-gather.17.cloned.1.call-update) | async-done | bytes 6553616 | tf_op jit(solution)/shard_map/all_gather | solution.py:40
  143.9 21.8 %fusion.19 = (f32[2048]{0:T(1024)S(1)}, bf16[2048,1024]{0,1:T(8,128)(2,1)}) fusion(bf16[2048,3200]{1,0:T(8,128)(2,1)} %get-tuple-element.30, bf16[1,3200,1024]{2,1,0:T(8,128)(2,1)} %all-gather.17.cloned.1.call-done, bf16[1,2048,1024]{1,2,0:T(8,128)(2,1)} %copy.20), kind=kOutput, calls=%fused_computation.37 | convolution fusion | flops 13432256512 | bytes 28057600 | tf_op jit(solution)/shard_map/dot_general | solution.py:10
  165.7 22.2 %all-gather.21.cloned.1.call-done = bf16[1,3200,1024]{2,1,0:T(8,128)(2,1)} async-done(((bf16[1,400,1024]{2,1,0:T(8,128)(2,1)}), bf16[1,3200,1024]{2,1,0:T(8,128)(2,1)}) %all-gather.21.cloned.1.call-update) | async-done | bytes 6553616 | tf_op jit(solution)/shard_map/all_gather | solution.py:40
  187.9 20.9 %convolution_convert_fusion.1 = bf16[2048,3200]{1,0:T(8,128)(2,1)} fusion(bf16[1,3200,1024]{2,1,0:T(8,128)(2,1)} %all-gather.21.cloned.1.call-done, bf16[1,2048,1024]{2,1,0:T(8,128)(2,1)} %param.12), kind=kOutput, calls=%fused_computation.23 | convolution fusion | flops 13428326400 | bytes 23855104 | tf_op jit(solution)/shard_map/transpose(jvp())/dot_general | solution.py:10
  208.8 23.1 %all-gather.23.cloned.1.call-done = bf16[1,1024,3200]{2,1,0:T(8,128)(2,1)} async-done(((bf16[1,128,3200]{2,1,0:T(8,128)(2,1)}), bf16[1,1024,3200]{2,1,0:T(8,128)(2,1)}) %all-gather.23.cloned.1.call-update) | async-done | bytes 6553616 | tf_op jit(solution)/shard_map/all_gather | solution.py:40
  231.9 22.8 %fusion.28 = f32[2048,3200]{1,0:T(8,128)} fusion(bf16[1,1024,3200]{2,1,0:T(8,128)(2,1)} %all-gather.23.cloned.1.call-done, bf16[2048,1024]{0,1:T(8,128)(2,1)} %get-tuple-element.33, f32[2048]{0:T(1024)S(1)} %fusion.80), kind=kOutput, calls=%fused_computation.46 | convolution fusion | flops 13428064256 | bytes 36970496 | tf_op jit(solution)/shard_map/jvp()/dot_general | solution.py:22
  254.7 21.2 %all-gather.19.cloned.1.call-done = bf16[1,1024,3200]{2,1,0:T(8,128)(2,1)} async-done(((bf16[1,128,3200]{2,1,0:T(8,128)(2,1)}), bf16[1,1024,3200]{2,1,0:T(8,128)(2,1)}) %all-gather.19.cloned.1.call-update) | async-done | bytes 6553616 | tf_op jit(solution)/shard_map/all_gather | solution.py:40
  275.9 38.7 %fusion.2 = (bf16[2048,3200]{1,0:T(8,128)(2,1)}, f32[2048,3200]{1,0:T(8,128)}) fusion(f32[2048,3200]{1,0:T(8,128)} %fusion.28, bf16[2048,3200]{1,0:T(8,128)(2,1)} %convolution_convert_fusion.1, bf16[1,1024,3200]{2,1,0:T(8,128)(2,1)} %all-gather.19.cloned.1.call-done, bf16[2048,1024]{0,1:T(8,128)(2,1)} %get-tuple-element.33, f32[2048]{0:T(1024)S(1)} %fusion.80), kind=kOutput, calls=%fused_computation.8 | convolution fusion | flops 13506707456 | bytes 89399296 | tf_op jit(solution)/shard_map/jvp()/dot_general | solution.py:21
  314.6 22.6 %fusion.12 = bf16[2048,1024]{0,1:T(8,128)(2,1)} fusion(bf16[2048,3200]{1,0:T(8,128)(2,1)} %convolution_convert_fusion.1, bf16[1,1024,3200]{2,1,0:T(8,128)(2,1)} %all-gather.23.cloned.1.call-done, f32[2048,3200]{1,0:T(8,128)} %get-tuple-element.35), kind=kOutput, calls=%fused_computation.21 | convolution fusion | flops 13461094400 | bytes 50069504 | tf_op jit(solution)/shard_map/transpose(jvp())/dot_general | solution.py:22
  337.2 21.8 %fusion.21 = (f32[2048]{0:T(1024)S(1)}, bf16[2048,1024]{0,1:T(8,128)(2,1)}) fusion(bf16[2048,1024]{0,1:T(8,128)(2,1)S(1)} %copy-done.6, bf16[2048,1024]{0,1:T(8,128)(2,1)} %fusion.12, bf16[2048,3200]{1,0:T(8,128)(2,1)} %get-tuple-element.34, bf16[1,1024,3200]{2,1,0:T(8,128)(2,1)} %all-gather.19.cloned.1.call-done), kind=kOutput, calls=%fused_computation.39 | convolution fusion | flops 13432256512 | bytes 32251904 | tf_op jit(solution)/shard_map/transpose(jvp())/dot_general | solution.py:21
  359.1 4.9 fusion.44
  364.0 2.0 copy-done.7
  366.0 19.5 %convolution_convert_fusion.2 = bf16[3200,1024]{1,0:T(8,128)(2,1)} fusion(bf16[2048,3200]{1,0:T(8,128)(2,1)} %get-tuple-element.30, bf16[2048,1024]{0,1:T(8,128)(2,1)S(1)} %fusion.44), kind=kOutput, calls=%fused_computation.44 | convolution fusion | flops 13425049600 | bytes 23855104 | tf_op jit(solution)/shard_map/transpose(jvp())/dot_general | solution.py:10
  385.5 26.0 %fusion.25 = bf16[3200,1024]{1,0:T(8,128)(2,1)} fusion(f32[2048,3200]{1,0:T(8,128)} %fusion.28, bf16[1,2048,1024]{2,1,0:T(8,128)(2,1)} %param.12, f32[2048,3200]{1,0:T(8,128)} %get-tuple-element.35), kind=kOutput, calls=%fused_computation.41 | convolution fusion | flops 13464371200 | bytes 63176704 | tf_op jit(solution)/shard_map/transpose(jvp())/dot_general | solution.py:10
  411.6 21.4 %convolution_convert_fusion = bf16[2048,3200]{1,0:T(8,128)(2,1)} fusion(bf16[2048,1024]{0,1:T(8,128)(2,1)} %copy-done.7, bf16[1,3200,1024]{2,1,0:T(8,128)(2,1)} %all-gather.17.cloned.1.call-done), kind=kOutput, calls=%fused_computation.22 | convolution fusion | flops 13428326400 | bytes 23855104 | tf_op jit(solution)/shard_map/transpose(jvp())/dot_general | solution.py:10
  433.1 24.3 %fusion.27 = bf16[1024,3200]{1,0:T(8,128)(2,1)} fusion(bf16[2048,3200]{1,0:T(8,128)(2,1)} %convolution_convert_fusion, f32[2048,3200]{1,0:T(8,128)} %fusion.41, bf16[1,2048,1024]{1,2,0:T(8,128)(2,1)S(1)} %copy-done.1, f32[2048]{0:T(1024)S(1)} %copy-done.20), kind=kOutput, calls=%fused_computation.43 | convolution fusion | flops 13470662656 | bytes 50077696 | tf_op jit(solution)/shard_map/transpose(jvp())/dot_general | solution.py:22
  457.5 0.6 copy-done.16
  458.1 25.5 %fusion.26 = bf16[1024,3200]{1,0:T(8,128)(2,1)} fusion(bf16[2048,3200]{1,0:T(8,128)(2,1)} %convolution_convert_fusion.1, bf16[2048,1024]{0,1:T(8,128)(2,1)} %get-tuple-element.33, f32[2048]{0:T(1024)S(1)} %copy-done.16, f32[2048,3200]{1,0:T(8,128)} %get-tuple-element.35), kind=kOutput, calls=%fused_computation.42 | convolution fusion | flops 13470662656 | bytes 50077696 | tf_op jit(solution)/shard_map/transpose(jvp())/dot_general | solution.py:22
  483.6 32.6 %fusion.22 = bf16[1024,3200]{1,0:T(8,128)(2,1)} fusion(f32[2048,3200]{1,0:T(8,128)} %fusion.41, f32[2048,3200]{1,0:T(8,128)} %get-tuple-element.31, bf16[2048,3200]{1,0:T(8,128)(2,1)} %convolution_convert_fusion, bf16[1,2048,1024]{1,2,0:T(8,128)(2,1)} %copy.20, f32[2048]{0:T(1024)S(1)} %copy-done.20), kind=kOutput, calls=%fused_computation.40 | convolution fusion | flops 13503430656 | bytes 76292096 | tf_op jit(solution)/shard_map/transpose(jvp())/dot_general | solution.py:21
  516.2 21.1 %convolution_convert_fusion.3 = bf16[1024,3200]{1,0:T(8,128)(2,1)} fusion(bf16[2048,3200]{1,0:T(8,128)(2,1)} %get-tuple-element.34, bf16[2048,1024]{0,1:T(8,128)(2,1)} %get-tuple-element.33, f32[2048]{0:T(1024)S(1)} %copy-done.16), kind=kOutput, calls=%fused_computation.45 | convolution fusion | flops 13428064256 | bytes 23863296 | tf_op jit(solution)/shard_map/transpose(jvp())/dot_general | solution.py:21
  537.5 28.8 %reduce-scatter.13.cloned.1.call-done = bf16[128,3200]{1,0:T(8,128)(2,1)} async-done(((bf16[1024,3200]{1,0:T(8,128)(2,1)}), bf16[128,3200]{1,0:T(8,128)(2,1)}) %reduce-scatter.13.cloned.1.call-update) | async-done | bytes 819216 | tf_op jit(solution)/shard_map/reduce_scatter | solution.py:43
  566.3 45.9 %reduce-scatter.7.cloned.1.call-done = bf16[128,3200]{1,0:T(8,128)(2,1)} async-done(((bf16[1024,3200]{1,0:T(8,128)(2,1)}), bf16[128,3200]{1,0:T(8,128)(2,1)}) %reduce-scatter.7.cloned.1.call-update) | async-done | bytes 819216 | tf_op jit(solution)/shard_map/reduce_scatter | solution.py:43
  612.2 45.8 %reduce-scatter.9.cloned.1.call-done = bf16[128,3200]{1,0:T(8,128)(2,1)} async-done(((bf16[1024,3200]{1,0:T(8,128)(2,1)}), bf16[128,3200]{1,0:T(8,128)(2,1)}) %reduce-scatter.9.cloned.1.call-update) | async-done | bytes 819216 | tf_op jit(solution)/shard_map/reduce_scatter | solution.py:43
  658.0 114.2 %all-reduce.3.cloned.1.call-done = (bf16[1,128,3200]{2,1,0:T(8,128)(2,1)}, bf16[1,128,3200]{2,1,0:T(8,128)(2,1)}, bf16[1,128,3200]{2,1,0:T(8,128)(2,1)}, bf16[1,...) async-done(((bf16[1,128,3200]{2,1,0:T(8,128)(2,1)}, bf16[1,128,3200]{2,1,0:T(8,128)(2,1)}, bf16[1,128,3200]{2,1,0:T(8,128)(2,1)}, ...) | async-done | bytes 4915216 | tf_op jit(solution)/shard_map/psum | solution.py:43
  772.2 2.8 fusion.62
  775.1 2.8 fusion.61
  777.9 2.8 fusion.60
  782.7 13.1 %psum.55 = f32[]{:T(128)} all-reduce(f32[]{:T(128)S(6)} %add.111), channel_id=1, replica_groups=mesh['rep'=1,'r'=16,'s'=8] {'s'}, use_global_device_ids=true, to_apply=%region_18.19 | all-reduce | flops 1 | bytes 8 | tf_op jit(solution)/shard_map/psum | solution.py:58
  796.6 7.4 fusion.68
  804.1 1.6 copy-done.12
  805.7 0.9 copy-done.13
  806.6 0.9 copy-done.14
  807.6 9.1 %fusion.59 = (bf16[2,128,3200]{2,1,0:T(8,128)(2,1)}, f32[2,128,3200]{2,1,0:T(8,128)}, f32[2,128,3200]{2,1,0:T(8,128)}, bf16[2,128,3200]{2,1,0:T(8,128)(2,1)}, f3...) fusion(bf16[2,128,3200]{2,1,0:T(8,128)(2,1)S(1)} %copy-done.4, f32[]{:T(128)S(6)} %min_shard_map.3, ...), kind=kLoop, calls=%fused_computation.89 | loop fusion | flops 32768000 | bytes 36044804 | tf_op jit(solution)/shard_map/convert_element_type | solution.py:30
  (64 shorter events, 0.8 us)
Async XLA Ops:
  7.2 5.7 copy-start.2
  7.2 48.4 %all-gather.13.cloned.1.call-start = ((), (), s32[]{:S(2)}) async-start(), calls=%async_computation.12 | async-start | bytes 7372800 | tf_op jit(solution)/shard_map/all_gather | solution.py:40
  10.0 89.7 %all-gather.15.cloned.1.call-start = ((), (), s32[]{:S(2)}) async-start(), calls=%async_computation.13 | async-start | bytes 7372800 | tf_op jit(solution)/shard_map/all_gather | solution.py:40
  12.8 131.1 %all-gather.17.cloned.1.call-start = ((), (), s32[]{:S(2)}) async-start(), calls=%async_computation.14 | async-start | bytes 7372800 | tf_op jit(solution)/shard_map/all_gather | solution.py:40
  14.2 173.7 %all-gather.21.cloned.1.call-start = ((), (), s32[]{:S(2)}) async-start(), calls=%async_computation.16 | async-start | bytes 7372800 | tf_op jit(solution)/shard_map/all_gather | solution.py:40
  14.7 217.2 %all-gather.23.cloned.1.call-start = ((), (), s32[]{:S(2)}) async-start(), calls=%async_computation.17 | async-start | bytes 7372800 | tf_op jit(solution)/shard_map/all_gather | solution.py:40
  15.3 260.6 %all-gather.19.cloned.1.call-start = ((), (), s32[]{:S(2)}) async-start(), calls=%async_computation.15 | async-start | bytes 7372800 | tf_op jit(solution)/shard_map/all_gather | solution.py:40
  15.9 521.5 %reduce-scatter.15.cloned.1.call-start = ((), (), s32[]{:S(2)}) async-start(), calls=%async_computation.10 | async-start | bytes 7372800 | tf_op jit(solution)/shard_map/reduce_scatter | solution.py:43
  25.5 74.2 %copy-start.19 = (f32[2048]{0:T(1024)}, f32[2048]{0:T(1024)S(1)}, u32[]{:S(2)}) copy-start(f32[2048]{0:T(1024)S(1)} %add_rsqrt_fusion) | copy-start | bytes 24580
  165.7 43.1 %copy-start.17 = (f32[2048]{0:T(1024)}, f32[2048]{0:T(1024)S(1)}, u32[]{:S(2)}) copy-start(f32[2048]{0:T(1024)S(1)} %get-tuple-element.32) | copy-start | bytes 24580
  165.7 193.3 %copy-start.15 = (f32[2048]{0:T(1024)}, f32[2048]{0:T(1024)S(1)}, u32[]{:S(2)}) copy-start(f32[2048]{0:T(1024)S(1)} %fusion.80) | copy-start | bytes 24580
  314.6 22.6 %copy-start.6 = (bf16[2048,1024]{0,1:T(8,128)(2,1)S(1)}, bf16[2048,1024]{0,1:T(8,128)(2,1)}, u32[]{:S(2)}) copy-start(bf16[2048,1024]{0,1:T(8,128)(2,1)} %get-tuple-element.33) | copy-start | bytes 12582916
  337.2 21.9 %copy-start.18 = (f32[2048]{0:T(1024)S(1)}, f32[2048]{0:T(1024)}, u32[]{:S(2)}) copy-start(f32[2048]{0:T(1024)} %copy-done.17) | copy-start | bytes 24580
  337.2 21.9 %copy-start = (bf16[1,2048,1024]{1,2,0:T(8,128)(2,1)S(1)}, bf16[1,2048,1024]{1,2,0:T(8,128)(2,1)}, u32[]{:S(2)}) copy-start(bf16[1,2048,1024]{1,2,0:T(8,128)(2,1)} %copy.21) | copy-start | bytes 12582916
  363.9 2.1 copy-start.7
  385.5 151.9 %reduce-scatter.17.cloned.1.call-start = ((), (), s32[]{:S(2)}) async-start(), calls=%async_computation.11 | async-start | bytes 7372800 | tf_op jit(solution)/shard_map/reduce_scatter | solution.py:43
  411.5 21.5 %copy-start.20 = (f32[2048]{0:T(1024)S(1)}, f32[2048]{0:T(1024)}, u32[]{:S(2)}) copy-start(f32[2048]{0:T(1024)} %copy-done.19) | copy-start | bytes 24580
  411.6 125.9 %reduce-scatter.11.cloned.1.call-start = ((), (), s32[]{:S(2)}) async-start(), calls=%async_computation.8 | async-start | bytes 7372800 | tf_op jit(solution)/shard_map/reduce_scatter | solution.py:43
  411.6 21.4 %copy-start.1 = (bf16[1,2048,1024]{1,2,0:T(8,128)(2,1)S(1)}, bf16[1,2048,1024]{1,2,0:T(8,128)(2,1)}, u32[]{:S(2)}) copy-start(bf16[1,2048,1024]{1,2,0:T(8,128)(2,1)} %copy.20) | copy-start | bytes 12582916
  457.4 0.7 copy-start.16
  457.4 108.9 %reduce-scatter.13.cloned.1.call-start = ((), (), s32[]{:S(2)}) async-start(), calls=%async_computation.9 | async-start | bytes 7372800 | tf_op jit(solution)/shard_map/reduce_scatter | solution.py:43
  483.6 128.6 %reduce-scatter.7.cloned.1.call-start = ((), (), s32[]{:S(2)}) async-start(), calls=%async_computation.6 | async-start | bytes 7372800 | tf_op jit(solution)/shard_map/reduce_scatter | solution.py:43
  516.2 141.8 %reduce-scatter.9.cloned.1.call-start = ((), (), s32[]{:S(2)}) async-start(), calls=%async_computation.7 | async-start | bytes 7372800 | tf_op jit(solution)/shard_map/reduce_scatter | solution.py:43
  537.3 259.1 %copy-start.3 = (bf16[2,400,1024]{2,1,0:T(8,128)(2,1)S(1)}, bf16[2,400,1024]{2,1,0:T(8,128)(2,1)}, u32[]{:S(2)}) copy-start(bf16[2,400,1024]{2,1,0:T(8,128)(2,1)} %param.15) | copy-start | bytes 4915204
  537.3 234.9 %all-reduce.3.cloned.1.call-start = ((), (), s32[]{:S(2)}) async-start(), calls=%async_computation.18 | async-start | bytes 9830400 | tf_op jit(solution)/shard_map/psum | solution.py:43
  796.5 7.5 copy-start.4
  796.5 7.5 copy-start.5
  796.5 7.5 copy-start.8
  796.5 7.5 copy-start.9
  796.5 7.5 copy-start.10
  796.5 7.5 copy-start.11
  796.5 9.1 %copy-start.12 = (f32[2,128,3200]{2,1,0:T(8,128)S(1)}, f32[2,128,3200]{2,1,0:T(8,128)}, u32[]{:S(2)}) copy-start(f32[2,128,3200]{2,1,0:T(8,128)} %param.19) | copy-start | bytes 9830404
  796.6 10.1 %copy-start.13 = (f32[2,128,3200]{2,1,0:T(8,128)S(1)}, f32[2,128,3200]{2,1,0:T(8,128)}, u32[]{:S(2)}) copy-start(f32[2,128,3200]{2,1,0:T(8,128)} %param.16) | copy-start | bytes 9830404
  796.6 11.0 %copy-start.14 = (f32[2,128,3200]{2,1,0:T(8,128)S(1)}, f32[2,128,3200]{2,1,0:T(8,128)}, u32[]{:S(2)}) copy-start(f32[2,128,3200]{2,1,0:T(8,128)} %param.20) | copy-start | bytes 9830404
Sparse Core Ops, SparseCore 0:
  10.3 45.2 all-gather.12
  57.8 41.8 all-gather.14
  102.0 41.8 all-gather.16
  146.0 41.8 all-gather.20
  190.0 41.8 all-gather.22
  234.0 41.8 all-gather.18
  385.6 43.0 reduce-scatter.14
  431.2 43.4 reduce-scatter.16
  477.1 43.4 reduce-scatter.10
  522.8 43.4 reduce-scatter.12
  568.7 43.4 reduce-scatter.6
  614.5 43.4 reduce-scatter.8
  662.2 110.0 all-reduce.2
where the time goes:
time: 832 us; the launch traced here: 823 us
  matrix products  373 us (45%)
  waiting for transfers between devices  361 us (43%)
  other arithmetic  33 us (4%)
  local copies, waits for them, and re-layouts  26.1 us (3%)
  between operations  17 us (2%)
  blocking collectives  13.1 us (2%)
    dot_general x5, matrix products, layer(): gate = jnp.dot(a, w['w_gate'], preferred_element_type=jnp.float32)  137 us
    dot_general x5, matrix products, layer(): up = jnp.dot(a, w['w_up'], preferred_element_type=jnp.float32)  126 us
    all_gather x6, waiting for transfers between devices, fetched(): lax.all_gather(w[number], 's', axis=0, tiled=True)  124 us
    reduce_scatter x6, waiting for transfers between devices, summed(): lax.psum_scatter(term, 's', scatter_dimension=0, tiled=True)  121 us
    psum x1, waiting for transfers between devices, summed(): lax.psum(lax.psum_scatter(term, 's', scatter_dimension=0, tiled=True), 'r')  114 us
    dot_general x5, matrix products, matmul(): jnp.dot(a, w, preferred_element_type=jnp.float32).astype(jnp.bfloat16)  110 us
    unnamed x44, local copies, waits for them, and re-layouts  19.3 us
  transfers between devices with their start and end apart: 13, of which 10 were waited for; matrix products, arithmetic and copies ran while one was open for 35% of the time, Pallas kernels for 0%

commit v1 on v0

v1 whole, which is shorter than its diff:
```python
import jax, jax.numpy as jnp
from jax import lax
from jax.experimental import pallas as pl
from jax.experimental.pallas import tpu as pltpu
from jax.sharding import PartitionSpec as P

bf, f32 = jnp.bfloat16, jnp.float32
T, D, F, TF = 2048, 1024, 3200, 640
TWO, MATS, RING = 2, 3, 4
NT = F // TF
NU = TWO * MATS * NT
NA = TWO * NT + TWO
DEEP = 6
LANES, SUB, HALF, CH, SH = 128, 80, 512, 256, 400
DEV = D // LANES
TF2, TF3, TB, TK = TWO * TF, MATS * TF, T // TWO, T // RING
AROWS = LANES // DEV
OFFS = range(1, RING)
VMEM_LIMIT = 67043328
EPS = 1e-6
OFFLAY = NU // TWO


def sds(s, d): return jax.ShapeDtypeStruct(s, d)
def dot_(a, b, ca, cb): return lax.dot_general(a, b, (((ca,), (cb,)), ((), ())), preferred_element_type=f32)
def mul(i, n): return pl.multiple_of(i * n, n)
def blk(i, n): return pl.ds(mul(i, n), n)
def cut(n): return pl.ds(0, n)
def cpy(src, dst, sem): return pltpu.make_async_copy(src, dst, sem)
def wt(ref, sem): cpy(ref, ref, sem).wait()
def start(cs):
    for q in cs: q.start()
def each(lo, hi, f):
    def g(i, _):
        f(i)
        return _
    lax.fori_loop(lo, hi, g, 0)
def rms(wide): return lax.rsqrt(jnp.mean(wide * wide, -1, keepdims=True) + EPS)
def pc(k): return (k % TWO) * RING + k // TWO
def par(u): return u % TWO
def ring(u): return u % RING


def step_kernel(x_h, dy_h, wg_i, wu_i, wd_i,
                gt_o, gd_o, sq_o, WGU, WD, a0p_h, h1p_h, AB_h, h_h,
                ya, acc, wgu, wdb, H, G, R0, Pb, R1, Q, R2, U, R3, GT, sqa, SQ,
                dysem, asem, psem, ownsem, gusem, wdsem, stsem, hsem, gtsem, locsem,
                s0s, s0r, s1s, s1r, s2s, s2r, s3s, s3r, s4s, s4r, a2s, a2r,
                ag0s, ag0r, agds, agdr, ag1s, ag1r, ag2s, ag2r, sqs, sqr):
    r_, me = lax.axis_index("r"), lax.axis_index("s")
    x, y, z, c = me // TWO, r_ // RING, r_ % RING, me % TWO
    own = c * RING + x
    def dev(x, y, z, c): return (0, y * RING + z, x * TWO + c)
    def xdev(d): return dev(ring(x + d), y, z, c)
    def ydev(d): return dev(x, ring(y + d), z, c)
    def zdev(d): return dev(x, y, ring(z + d), c)
    part = dev(x, y, z, 1 - c)
    AX = ((0, y, ydev), (1, z, zdev))
    dyp, ap = ya.at[0], ya.at[1]
    bar = pltpu.get_barrier_semaphore()
    peers = [part] + [f(d) for f in (xdev, ydev, zdev) for d in OFFS] + [dev(ring(x + d), y, z, 1 - c) for d in OFFS]
    for p in peers: pl.semaphore_signal(bar, inc=1, device_id=p, device_id_type=pl.DeviceIdType.MESH)
    def rd(src, dst, ss, rs, d):
        return pltpu.make_async_remote_copy(src_ref=src, dst_ref=dst, send_sem=ss, recv_sem=rs, device_id=d, device_id_type=pl.DeviceIdType.MESH)
    def same(ref, ss, rs, d): return rd(ref, ref, ss, rs, d)
    def permuted(src, dst, sem): return [cpy(src.at[:, pl.ds(k * LANES, LANES)], dst.at[:, pl.ds(pc(k) * LANES, LANES)], sem) for k in range(DEV)]
    start(permuted(x_h, ap, psem))
    staged = [wdb.at[pl.ds(l * TF, SH)] for l in range(TWO)]
    for l in range(TWO): start(permuted(wd_i.at[l], staged[l], ownsem.at[l]))
    start(permuted(dy_h, dyp, dysem))
    sqa[...] = jnp.zeros_like(sqa)
    for l in range(TWO):
        wt(staged[l], ownsem.at[l])
        cpy(staged[l], WD.at[l, blk(me, SH), :], ownsem.at[l]).start()
    pl.semaphore_wait(bar, len(peers))

    def gu_load(l, j, b):
        for m, inp in enumerate((wg_i, wu_i)):
            cols = pl.ds(m * TF, TF)
            cpy(inp.at[l, :, blk(j, TF)], wgu.at[b, blk(own, LANES), cols], gusem.at[b]).start()
            def one(e):
                k = (own + e) % DEV
                cpy(WGU.at[l, k, m, :, blk(j, TF)], wgu.at[b, blk(k, LANES), cols], gusem.at[b]).start()
            each(1, DEV, one)
    def gu_wait(b): wt(wgu.at[b], gusem.at[b])
    def d_load(l, j, b): cpy(WD.at[l, blk(j, TF), :], wdb.at[blk(b, TF)], wdsem.at[b]).start()
    def d_wait(b): wt(wdb.at[blk(b, TF)], wdsem.at[b])

    def q16(h, q): return pl.ds(pl.multiple_of(h * (LANES // TWO) + q * AROWS, AROWS), AROWS)
    def colq(h, q): return blk(pc(RING * h + q), LANES)
    def fork(u, fg, fd):
        @pl.when(u % (NT + TWO) < NT)
        def _(): fg(u // (NT + TWO), u % (NT + TWO))
        @pl.when(u % (NT + TWO) >= NT)
        def _(): fd(u - NT)
    def wait6(ref, ss, rs, b):
        def one(i):
            h, d = i // MATS, i % MATS
            wt(ref, ss.at[b, h, d])
            wt(ref, rs.at[b, h, d])
        each(0, DEEP, one)
    def A0(u):
        b = u % DEEP
        def fg(l, j):
            for m, inp in enumerate((wg_i, wu_i)):
                def one(i):
                    for h, q, _ in AX: rd(inp.at[l, q16(h, q), blk(j, TF)], WGU.at[l, own, m, q16(h, q), blk(j, TF)], ag0s.at[b, h, i], ag0r.at[b, h, i], xdev(i + 1)).start()
                each(0, MATS, one)
                rd(inp.at[l, :, blk(j, TF)], WGU.at[l, own, m, :, blk(j, TF)], agds.at[u], agdr.at[u], part).start()
        def fd(l):
            wt(WD.at[0, cut(SH), :], ownsem.at[l])
            def one(i):
                for h, q, _ in AX: same(WD.at[l, blk(me, SH), colq(h, q)], ag0s.at[b, h, i], ag0r.at[b, h, i], xdev(i + 1)).start()
            each(0, MATS, one)
            same(WD.at[l, blk(me, SH), :], agds.at[u], agdr.at[u], part).start()
        fork(u, fg, fd)
    def A1(u):
        b = u % DEEP
        def fg(l, j):
            wait6(WGU.at[0, 0, :, cut(AROWS), cut(TF)], ag0s, ag0r, b)
            def one(i):
                k, d = c * RING + ring(x + i // MATS + 1), i % MATS
                for h, q, f in AX: same(WGU.at[l, k, :, q16(h, q), blk(j, TF)], ag1s.at[b, h, d], ag1r.at[b, h, d], f(d + 1)).start()
            each(0, MATS * MATS, one)
        def fd(l):
            wait6(WD.at[0, cut(SH), cut(LANES)], ag0s, ag0r, b)
            def one(i):
                k, d = TWO * ring(x + i // MATS + 1) + c, i % MATS
                for h, q, f in AX: same(WD.at[l, blk(k, SH), colq(h, q)], ag1s.at[b, h, d], ag1r.at[b, h, d], f(d + 1)).start()
            each(0, MATS * MATS, one)
        fork(u, fg, fd)
    gu1, gu3 = WGU.at[0, 0, :, :, cut(TF)], WGU.at[0, cut(MATS), :, :, cut(TF)]
    wd1, wd3 = WD.at[0, cut(SH), :], WD.at[0, cut(MATS * SH), :]
    def A2(u):
        b = u % DEEP
        def fg(l, j):
            wait6(WGU.at[0, cut(MATS), :, cut(AROWS), cut(TF)], ag1s, ag1r, b)
            each(1, RING, lambda i: same(WGU.at[l, c * RING + ring(x + i), :, :, blk(j, TF)], ag2s.at[b], ag2r.at[u], part).start())
        def fd(l):
            wait6(WD.at[0, cut(MATS * SH), cut(LANES)], ag1s, ag1r, b)
            each(1, RING, lambda i: same(WD.at[l, blk(TWO * ring(x + i) + c, SH), :], ag2s.at[b], ag2r.at[u], part).start())
        fork(u, fg, fd)
    def A3(u):
        b = u % DEEP
        def done(one, three):
            for ref, sem in ((one, agds.at[u]), (one, agdr.at[u]), (three, ag2s.at[b]), (three, ag2r.at[u])): wt(ref, sem)
        fork(u, lambda l, j: done(gu1, gu3), lambda l: done(wd1, wd3))
    def guard(A, u):
        @pl.when(jnp.logical_and(u >= 0, u < NA))
        def _(): A(u)

    def c0(u): return rd(G.at[par(u), :, blk(1 - c, HALF)], R0.at[ring(u)], s0s.at[par(u)], s0r.at[ring(u)], part)
    def c1(u):
        return [rd(Pb.at[par(u), h, ring(q + d)], R1.at[ring(u), h, d - 1], s1s.at[par(u), h, d - 1], s1r.at[ring(u), h, d - 1], f(d)) for d in OFFS for h, q, f in AX]
    def c2(u): return [rd(Q.at[par(u), ring(x + d)], R2.at[ring(u), d - 1], s2s.at[par(u), d - 1], s2r.at[ring(u), d - 1], xdev(d)) for d in OFFS]
    def c3(u, recv):
        o = []
        for d in OFFS:
            for h, q, f in ((0, z, zdev), (1, y, ydev)):
                k = ring(q + d) if recv else q
                o.append(rd(U.at[par(u), h], R3.at[ring(u), h, k], s3s.at[par(u), h, d - 1], s3r.at[ring(u), h, k], f(d)))
        return o
    def rows(h, q): return pl.ds(pl.multiple_of(h * (TF // TWO) + q * SUB, SUB), SUB)
    def c4(u):
        return [same(GT.at[u, rows(h, q)], s4s.at[par(u), h, d - 1], s4r.at[ring(u), h, d - 1], f(d)) for d in OFFS for h, q, f in AX]
    def S0(u): c0(u).start()
    def S1(u):
        c0(u).wait()
        def one(i):
            for k in range(RING):
                mine = G[par(u), blk(i, SUB), blk(c * RING + k, LANES)]
                Pb[par(u), i // RING, ring(i), k] = (mine.astype(f32) + R0[ring(u), blk(i, SUB), pl.ds(k * LANES, LANES)].astype(f32)).astype(bf)
        each(0, DEV, one)
        start(c1(u))
    def S2(u):
        for q in c1(u): q.wait()
        for h, mine, _ in AX:
            for k in range(RING):
                s = Pb[par(u), h, mine, k].astype(f32)
                for d in range(MATS): s = s + R1[ring(u), h, d, k].astype(f32)
                Q[par(u), k, h] = s.astype(bf)
        start(c2(u))
    def S3(u):
        for q in c2(u): q.wait()
        for h in range(TWO):
            s = Q[par(u), x, h].astype(f32)
            for d in range(MATS): s = s + R2[ring(u), d, h].astype(f32)
            U[par(u), h] = s.astype(bf)
        start(c3(u, False))
    def S4(u):
        for q in c3(u, False): q.wait_send()
        for q in c3(u, True): q.wait_recv()
        R3[ring(u), 0, z] = U[par(u), 0]
        R3[ring(u), 1, y] = U[par(u), 1]
        for h, q, _ in AX:
            s = R3[ring(u), h, 0].astype(f32)
            for d in OFFS: s = s + R3[ring(u), h, d].astype(f32)
            GT[u, rows(h, q)] = s.astype(bf)
        start(c4(u))
    def a2a(u, i):
        lay, n = u // OFFLAY, DEV * ((u % OFFLAY) // MATS) + i
        src, dst = GT.at[u, blk(i, SUB)], gd_o.at[1 - lay, blk(n % NT, SUB), blk(me, LANES)]
        return n // NT, rd(src, dst, a2s, a2r.at[lay], (0, r_, n // NT)), cpy(src, dst, locsem)
    def S5(u):
        for q in c4(u): q.wait()
        v = GT[u].astype(f32)
        sqa[...] += jnp.sum((v * v).reshape(SUB, DEV, LANES), axis=0)
        @pl.when(u % MATS > 0)
        def _(): cpy(GT.at[u], gt_o.at[u], gtsem).start()
        @pl.when(u % MATS == 0)
        def _():
            def one(i):
                @pl.when(a2a(u, i)[0] != me)
                def _(): a2a(u, i)[1].start()
                @pl.when(a2a(u, i)[0] == me)
                def _(): a2a(u, i)[TWO].start()
            each(0, DEV, one)
    STAGES = (S5, S4, S3, S2, S1)
    def slot(t):
        for i, S in enumerate(STAGES):
            u = t - TWO * (len(STAGES) - i)
            @pl.when(jnp.logical_and(u >= 0, u < NU))
            def _(): S(u)

    each(0, MATS, A0)
    wt(ap, psem)
    def xnorm(i):
        wide = ya[1, blk(i, CH), :].astype(f32)
        ya[1, blk(i, CH), :] = (wide * rms(wide)).astype(bf)
    each(0, T // CH, xnorm)
    cpy(ap, a0p_h, asem).start()
    def head(i):
        guard(A2, i - 1)
        @pl.when(i == 0)
        def _(): A1(i)
        A1(i + 1)
        A0(i + MATS)
    each(0, TWO, head)
    each(0, 1, A3)
    gu_load(0, 0, 0)
    each(MATS, RING, A1)
    each(NT, DEEP, A0)
    def stv(i): return acc.at[blk(i, TF), :]
    def step1(j):
        b = par(j)
        gu_wait(b)
        hs = j % MATS
        hr = blk(hs, TF)
        @pl.when(j >= MATS)
        def _(): wt(H.at[cut(TF)], hsem.at[hs])
        def sub(s):
            i = j * RING + s
            k = i % MATS
            @pl.when(i >= MATS)
            def _(): wt(stv(0), stsem.at[k])
            gu = dot_(wgu[b], ya[1, blk(s, TK), :], 0, 1)
            g, u = gu[:TF], gu[TF:]
            sg = jax.nn.sigmoid(g)
            si = g * sg
            acc[blk(k, TF), 0:TK] = si
            acc[blk(k, TF), TK:] = u * (sg + si * (1 - sg))
            H[hr, blk(s, TK)] = (si * u).astype(bf)
            cpy(stv(k), AB_h.at[i], stsem.at[k]).start()
            @pl.when(s == 0)
            def _(): guard(A2, j + 1)
            @pl.when(s == TWO)
            def _():
                guard(A3, j + 1)
                @pl.when(j < NT - 1)
                def _(): gu_load(0, j + 1, 1 - b)
                @pl.when(j == NT - 1)
                def _(): cpy(WD.at[0, pl.ds(TF3, TF2), :], wdb, wdsem.at[TWO]).start()
                guard(A1, j + RING)
                guard(A0, j + DEEP)
        each(0, RING, sub)
        cpy(H.at[hr], h_h.at[blk(j, TF), :], hsem.at[hs]).start()
    each(0, NT, step1)
    for i in range(MATS): wt(stv(0), stsem.at[i])
    wt(ap, asem)
    start(permuted(x_h, ap, psem))
    lo, mid = cut(TF2), wgu.at[0, cut(TF), cut(D)]
    cpy(WD.at[0, pl.ds(TF2, TF), :], mid, wdsem.at[0]).start()
    acc[...] = jnp.zeros_like(acc)
    def down(i):
        @pl.when(i == 1)
        def _(): wt(H.at[lo], hsem.at[MATS])
        wt(wdb, wdsem.at[TWO])
        def halves(h): acc[blk(h, TB), :] += dot_(H[lo, blk(h, TB)], wdb[...], 0, 0)
        each(0, TWO, halves)
        @pl.when(i == 0)
        def _():
            for k in range(TWO): wt(H.at[cut(TF)], hsem.at[k])
            cpy(h_h.at[lo], H.at[lo], hsem.at[MATS]).start()
            cpy(WD.at[0, lo, :], wdb, wdsem.at[TWO]).start()
            A2(i + DEEP)
            A1(i + NA - MATS)
            A0(i + NA - 1)
            wt(mid, wdsem.at[0])
            def halves(h): acc[blk(h, TB), :] += dot_(H[TF2:TF3, blk(h, TB)], wgu[0, 0:TF, 0:D], 0, 0)
            each(0, TWO, halves)
        A3(i + DEEP)
        A2(i + DEEP + 1)
        @pl.when(i == 0)
        def _(): A1(i + NA - TWO)
    each(0, TWO, down)
    gu_load(1, 0, 1)
    d_load(1, 0, 0)
    wt(H.at[cut(TF)], hsem.at[TWO])
    wt(ap, psem)
    def h1s(b): return G.at[b, cut(CH)]
    def fin(i):
        b, r = par(i), blk(i, CH)
        @pl.when(i >= TWO)
        def _(): wt(h1s(0), hsem.at[b])
        h1 = (ya[1, r, :].astype(f32) + acc[r, :].astype(bf).astype(f32)).astype(bf)
        G[b, 0:CH] = h1
        cpy(h1s(b), h1p_h.at[r], hsem.at[b]).start()
        wide = h1.astype(f32)
        ya[1, r, :] = (wide * rms(wide)).astype(bf)
        acc[r, :] = jnp.zeros((CH, D), f32)
    each(0, T // CH, fin)
    for b in range(TWO): wt(h1s(0), hsem.at[b])
    def after(i):
        A3(i)
        A1(i + MATS)
    each(DEEP + TWO, DEEP + MATS, after)
    wt(dyp, dysem)

    def h1l(k): return cpy(h1p_h.at[pl.ds(k * D, D)], H.at[cut(D), pl.ds(k * D, D)], hsem.at[k])
    def abl(i): return cpy(AB_h.at[i], stv(i % MATS), stsem.at[i % MATS])
    def hload(j): return cpy(h_h.at[blk(j, TF), :], H.at[cut(TF)], hsem.at[TWO])
    def layer1(k, b):
        gu_wait(b)
        @pl.when(k + 1 < NT)
        def _(): gu_load(1, k + 1, 1 - b)
        def half(h):
            t = blk(h, TB)
            gu = dot_(wgu[b], ya[1, t, :], 0, 1)
            g, u = gu[:TF], gu[TF:]
            dh = dot_(wdb[blk(par(k), TF)], ya[0, t, :], 1, 1).astype(bf).astype(f32)
            sg = jax.nn.sigmoid(g)
            si = g * sg
            H[0:TF, t] = (si * u).astype(bf)
            H[TF2:TF3, t] = (dh * si).astype(bf)
            H[TF:TF2, t] = (dh * u * (sg + si * (1 - sg))).astype(bf)
            @pl.when(h == 0)
            def _(): guard(A2, k + DEEP + MATS)
        each(0, TWO, half)
        guard(A3, k + DEEP + MATS)
    def between():
        cpy(a0p_h, ap, asem).start()
        for k in range(TWO): wt(H.at[cut(D), cut(D)], hsem.at[k])
        def nb(i):
            r = blk(i, CH)
            wide = H[blk(ring(i), CH), blk(i // RING, D)].astype(f32)
            scale = rms(wide)
            da = acc[r, :].astype(bf).astype(f32)
            inner = jnp.mean(da * wide, -1, keepdims=True)
            dw = (da * scale - wide * (scale * scale * scale * inner)).astype(bf)
            ya[0, r, :] = (ya[0, r, :].astype(f32) + dw.astype(f32)).astype(bf)
        each(0, T // CH, nb)
        for i in range(TWO): abl(i).start()
        hload(0).start()
        wt(ap, asem)
    def layer0(j, b):
        def sub(s):
            i = j * RING + s
            @pl.when(i + TWO < NT * RING)
            def _(): abl(i + TWO).start()
            abl(i).wait()
            t, r = blk(s, TK), blk(i % MATS, TF)
            dh = dot_(wdb[blk(b, TF)], ya[0, t, :], 1, 1).astype(bf).astype(f32)
            H[TF2:TF3, t] = (dh * acc[r, 0:TK]).astype(bf)
            H[TF:TF2, t] = (dh * acc[r, TK:]).astype(bf)
        each(0, RING, sub)
        hload(j).wait()
    def tile(k):
        b, gb = par(k), par(k + 1)
        d_wait(b)
        @pl.when(k + 1 < NT)
        def _(): d_load(1, k + 1, 1 - b)
        @pl.when(jnp.logical_and(k + 1 >= NT, k + 1 < TWO * NT))
        def _(): d_load(0, k + 1 - NT, 1 - b)
        @pl.when(k < NT)
        def _(): layer1(k, gb)
        @pl.when(k == NT)
        def _(): between()
        @pl.when(k >= NT)
        def _(): layer0(k - NT, b)
        def mat(m):
            t = MATS * k + m
            slot(t)
            G[par(t)] = dot_(H[blk(m, TF)], ya[(m + 1) // TWO], 1, 0).astype(bf)
            S0(t)
            @pl.when(jnp.logical_and(k < NT, m < TWO))
            def _(): acc[blk(m, TB), :] += dot_(H[TF:TF3, blk(m, TB)], wgu[gb], 0, 1)
            @pl.when(jnp.logical_and(k == NT - 1, m == 1))
            def _():
                for q in range(TWO): h1l(q).start()
            @pl.when(jnp.logical_and(jnp.logical_and(k >= NT, k + 1 < TWO * NT), m == 0))
            def _(): hload(k - NT + 1).start()
        each(0, MATS, mat)
    each(0, TWO * NT, tile)
    each(NU, NU + TWO * len(STAGES), slot)

    SQ[me] = sqa[...]
    def sqc(e, i): return rd(sqa, SQ.at[i], sqs.at[e - 1], sqr.at[i], (0, r_, (me + e) % DEV))
    for e in range(1, DEV): sqc(e, me).start()
    def drain(n, k, sem): wt(GT.at[cut(n), cut(k)], sem)
    drain(NU - TWO * NT, TF, gtsem)
    drain(TWO, SH, locsem)
    drain(TWO * (DEV - 1), SH, a2s)
    for l in range(TWO): drain(DEV - 1, SH, a2r.at[l])
    for e in range(1, DEV):
        sqc(e, me).wait_send()
        sqc(e, (me + e) % DEV).wait_recv()
    tot = SQ[0]
    for i in range(1, DEV): tot = tot + SQ[i]
    sq_o[...] = tot


def train(x, dy, wg, wu, wd):
    hbm = pl.BlockSpec(memory_space=pl.ANY)
    V, S = pltpu.VMEM, pltpu.SemaphoreType.DMA
    b = (SUB, LANES)
    p3, r3, d3 = (TWO, TWO, MATS), (RING, TWO, MATS), (DEEP, TWO, MATS)
    one, two, three = S, S((TWO,)), S((MATS,))
    outs = [sds((NU, TF, LANES), bf), sds((TWO, SH, D), bf), sds((DEV, LANES), f32), sds((TWO, DEV, TWO, LANES, F), bf), sds((TWO, F, D), bf),
            sds((T, D), bf), sds((T, D), bf), sds((NT * RING, TF, D), f32), sds((F, T), bf)]
    specs = [hbm] * len(outs)
    specs[TWO] = pl.BlockSpec(memory_space=pltpu.VMEM)
    return pl.pallas_call(
        step_kernel,
        out_shape=outs, in_specs=[hbm] * (MATS + TWO), out_specs=specs,
        scratch_shapes=[
            V((TWO, T, D), bf), V((T, D), f32), V((TWO, D, TF2), bf), V((TF2, D), bf), V((TF3, T), bf), V((TWO, TF, D), bf), V((RING, TF, HALF), bf),
            V((TWO, TWO, RING, RING) + b, bf), V(r3 + (RING,) + b, bf), V((TWO, RING, TWO) + b, bf), V((RING, MATS, TWO) + b, bf), V((TWO, TWO) + b, bf), V((RING, TWO, RING) + b, bf),
            V((NU, TF, LANES), bf), V((DEV, LANES), f32), V((DEV, DEV, LANES), f32),
            one, one, one, two, two, three, three, S((RING,)), one, one,
            two, S((RING,)), S(p3), S(r3), S((TWO, MATS)), S((RING, MATS)), S(p3), S((RING, TWO, RING)), S(p3), S(r3), one, two,
            S(d3), S(d3), S((NA,)), S((NA,)), S(d3), S(d3), S((DEEP,)), S((NA,)), S((DEV - 1,)), S((DEV,))],
        compiler_params=pltpu.CompilerParams(collective_id=0, has_side_effects=True, vmem_limit_bytes=VMEM_LIMIT),
        name="train")(x, dy, wg, wu, wd)


def optimizer(sq, GT, GD, w, m, v):
    def kernel(sq, gg, gu, gd, *r):
        tot = jnp.sum(jnp.sum(sq[...], axis=0, keepdims=True), axis=1, keepdims=True)
        factor = jnp.minimum(1.0, 0.5 * lax.rsqrt(tot / (TWO * MATS * D * F) + 1e-30))
        ws, ms, vs, wo, mo, vo = (r[i * MATS:(i + 1) * MATS] for i in range(TWO * MATS))
        for i, block in enumerate((gg, gu, gd)):
            g = block[0].astype(f32)
            g = (g if i == TWO else g.T) * factor
            mm = 0.9 * ms[i][0] + 0.1 * g
            vv = 0.95 * vs[i][0] + 0.05 * g * g
            ww = ws[i][0].astype(f32)
            wo[i][0] = (ww - 0.02 * (mm * lax.rsqrt(vv + 1e-8) + 0.1 * ww)).astype(bf)
            mo[i][0], vo[i][0] = mm, vv
    def tile(i): return pl.BlockSpec((1, TF, LANES), lambda l, j: ((1 - l) * OFFLAY + MATS * j + i, 0, 0))
    a, d = pl.BlockSpec((1, LANES, TF), lambda l, j: (l, 0, j)), pl.BlockSpec((1, SUB, D), lambda l, j: (l, j, 0))
    outs = tuple(sds(q.shape, t) for t in (bf, f32, f32) for q in w)
    return pl.pallas_call(
        kernel, grid=(TWO, NT), in_specs=[pl.BlockSpec((DEV, LANES), lambda l, j: (0, 0)), tile(1), tile(TWO), d] + [a, a, d] * MATS,
        out_specs=(a, a, d) * MATS, out_shape=outs,
        compiler_params=pltpu.CompilerParams(vmem_limit_bytes=VMEM_LIMIT, dimension_semantics=("arbitrary",) * TWO),
        name="optimizer")(sq, GT, GT, GD, *w, *m, *v)


def solution(mesh):
    def step(x, dy, *arrays):
        w, m, v = (arrays[i:i + MATS] for i in range(0, len(arrays), MATS))
        GT, GD, sq = train(x[0], dy[0], *w)[:MATS]
        return optimizer(sq, GT, GD, w, m, v)
    states, cuts = P(("rep", "r", "s"), None, None), P(None, "s", None)
    return jax.shard_map(step, mesh=mesh, in_specs=(states, states) + (cuts,) * (MATS * MATS), out_specs=(P("rep", "s", None),) * (MATS * MATS), check_vma=False)
```

time: 832 us -> 373 us (0.45); the launches traced: 823 us -> 373 us
  matrix products: 373 us -> 0 us
  Pallas kernels: 0 us -> 372 us
  waiting for transfers between devices: 361 us -> 0 us
  other arithmetic: 33 us -> 0 us
  local copies, waits for them, and re-layouts: 26.1 us -> 0 us
  between operations: 17 us -> 0.81 us
  blocking collectives: 13.1 us -> 0 us
    dot_general x15 -> x0, matrix products: 373 us -> none  [the longest x5 137 us: layer(): gate = jnp.dot(a, w['w_gate'], preferred_element_type=jnp.float32)]
    pallas_call x0 -> x2, Pallas kernels: none -> 372 us  [the longest x1 352 us: train(): pl.pallas_call(step_kernel, out_shape=outs, in_specs=[hbm] * (MATS + TWO)...]
    all_gather x6 -> x0, waiting for transfers between devices: 124 us -> none  [fetched(): lax.all_gather(w[number], 's', axis=0, tiled=True)]
    reduce_scatter x6 -> x0, waiting for transfers between devices: 121 us -> none  [summed(): lax.psum_scatter(term, 's', scatter_dimension=0, tiled=True)]
    psum x1 -> x0, waiting for transfers between devices: 114 us -> none  [summed(): lax.psum(lax.psum_scatter(term, 's', scatter_dimension=0, tiled=True), 'r')]
    unnamed x44 -> x0, local copies, waits for them, and re-layouts: 19.3 us -> none
    convert_element_type x2 -> x0, other arithmetic: 16.5 us -> none  [adamw(): return ((w - 0.02 * step).astype(jnp.bfloat16), m, v)]
    psum x1 -> x0, blocking collectives: 13.1 us -> none  [step(): squares = lax.psum(sum((jnp.sum(g * g) for g in gradients)), 's')]
  transfers between devices with their start and end apart: 13 -> 0, of which waited for: 10 -> 0; matrix products, arithmetic and copies ran while one was open for 35% -> 0% of each run, Pallas kernels for 0% -> 0%
where the time goes in v1:
time: 373 us
  Pallas kernels  372 us (100%)
    pallas_call x1, Pallas kernels, train(): pl.pallas_call(step_kernel, out_shape=outs, in_specs=[hbm] * (MATS + TWO)...  352 us
    pallas_call x1, Pallas kernels, optimizer(): pl.pallas_call(kernel, grid=(TWO, NT), in_specs=[pl.BlockSpec((DEV, LANES...  20.2 us

profile of v1, /device:TPU:1, one launch (start us, length us, event | category | flops | bytes accessed | tf_op | source)
XLA Modules:
  0.0 373.1 jit_solution(12700162635355661303)
XLA Ops:
  0.6 352.1 %train.1 = (bf16[30,640,128]{2,1,0:T(8,128)(2,1)}, bf16[2,400,1024]{2,1,0:T(8,128)(2,1)}, f32[8,128]{1,0:T(8,128)}, bf16[2,8,2,128,3200]{4,3,2,1,0:T(8,128)(2,1)...) custom-call(bf16[2048,1024]{1,0:T(8,128)(2,1)} %bitcast.2, ...), custom_call_target="tpu_custom_call" | custom-call | tf_op jit(solution)/shard_map/train/pallas_call | solution.py:432
  352.7 20.2 %optimizer.1 = (bf16[2,128,3200]{2,1,0:T(8,128)(2,1)}, bf16[2,128,3200]{2,1,0:T(8,128)(2,1)}, bf16[2,400,1024]{2,1,0:T(8,128)(2,1)}, f32[2,128,3200]{2,1,0:T(8,1...) custom-call(f32[8,128]{1,0:T(8,128)} %get-tuple-element.12.sq, ...), custom_call_target="tpu_custom_call" | custom-call | tf_op jit(solution)/shard_map/optimizer/pallas_call | solution.py:462

commit v2 on v1

--- a/solution.py
+++ b/solution.py
@@ -12,8 +12,10 @@
 NA = TWO * NT + TWO
 DEEP = 6
 LANES, SUB, HALF, CH, SH = 128, 80, 512, 256, 400
+NCH = 2
 DEV = D // LANES
-TF2, TF3, TB, TK = TWO * TF, MATS * TF, T // TWO, T // RING
+TF2, TF3, TB = TWO * TF, MATS * TF, T // TWO
+TC = TB // NCH
 AROWS = LANES // DEV
 OFFS = range(1, RING)
 VMEM_LIMIT = 67043328
@@ -69,9 +71,6 @@
     for l in range(TWO): start(permuted(wd_i.at[l], staged[l], ownsem.at[l]))
     start(permuted(dy_h, dyp, dysem))
     sqa[...] = jnp.zeros_like(sqa)
-    for l in range(TWO):
-        wt(staged[l], ownsem.at[l])
-        cpy(staged[l], WD.at[l, blk(me, SH), :], ownsem.at[l]).start()
     pl.semaphore_wait(bar, len(peers))
 
     def gu_load(l, j, b):
@@ -150,9 +149,19 @@
         def _(): A(u)
 
     def c0(u): return rd(G.at[par(u), :, blk(1 - c, HALF)], R0.at[ring(u)], s0s.at[par(u)], s0r.at[ring(u)], part)
+    def mat_(u): return u % MATS
+    def deep(u): return u % DEEP
     def c1(u):
-        return [rd(Pb.at[par(u), h, ring(q + d)], R1.at[ring(u), h, d - 1], s1s.at[par(u), h, d - 1], s1r.at[ring(u), h, d - 1], f(d)) for d in OFFS for h, q, f in AX]
-    def c2(u): return [rd(Q.at[par(u), ring(x + d)], R2.at[ring(u), d - 1], s2s.at[par(u), d - 1], s2r.at[ring(u), d - 1], xdev(d)) for d in OFFS]
+        return [rd(Pb.at[mat_(u), h, ring(q + d)], R1.at[ring(u), h, d - 1], s1s.at[ring(u), h, d - 1], s1r.at[ring(u), h, d - 1], f(d)) for d in OFFS for h, q, f in AX]
+    def c1x(u): return [rd(Pb.at[mat_(u), :, :, ring(x + d)], R1.at[ring(u), :, d - 1], s1s.at[ring(u), 0, d - 1], s1r.at[ring(u), 0, d - 1], xdev(d)) for d in OFFS]
+    def c2(u): return [rd(Q.at[par(u), ring(x + d)], R2.at[deep(u), d - 1], s2s.at[par(u), 0, d - 1], s2r.at[deep(u), 0, d - 1], xdev(d)) for d in OFFS]
+    def c2x(u):
+        return [rd(Q.at[par(u), ring(q + d), h], R2.at[deep(u), d - 1, h], s2s.at[par(u), h, d - 1], s2r.at[deep(u), h, d - 1], f(d)) for d in OFFS for h, q, f in AX]
+    def either(u, f, *args):
+        @pl.when(mat_(u) > 0)
+        def _(): f(*args[0])
+        @pl.when(mat_(u) == 0)
+        def _(): f(*args[1])
     def c3(u, recv):
         o = []
         for d in OFFS:
@@ -169,23 +178,29 @@
         def one(i):
             for k in range(RING):
                 mine = G[par(u), blk(i, SUB), blk(c * RING + k, LANES)]
-                Pb[par(u), i // RING, ring(i), k] = (mine.astype(f32) + R0[ring(u), blk(i, SUB), pl.ds(k * LANES, LANES)].astype(f32)).astype(bf)
+                Pb[mat_(u), i // RING, ring(i), k] = (mine.astype(f32) + R0[ring(u), blk(i, SUB), pl.ds(k * LANES, LANES)].astype(f32)).astype(bf)
         each(0, DEV, one)
-        start(c1(u))
+        either(u, lambda way: start(way(u)), (c1,), (c1x,))
+    def added(first, rest):
+        s = first.astype(f32)
+        for q in rest: s = s + q.astype(f32)
+        return s.astype(bf)
+    def second(u, got, first, send):
+        for q in got(u): q.wait()
+        for h, mine, _ in AX:
+            for k in range(RING): Q[par(u), k, h] = added(first(h, mine, k), [R1[ring(u), h, d, k] for d in range(MATS)])
+        start(send(u))
     def S2(u):
-        for q in c1(u): q.wait()
-        for h, mine, _ in AX:
-            for k in range(RING):
-                s = Pb[par(u), h, mine, k].astype(f32)
-                for d in range(MATS): s = s + R1[ring(u), h, d, k].astype(f32)
-                Q[par(u), k, h] = s.astype(bf)
-        start(c2(u))
+        @pl.when(mat_(u) > 0)
+        def _(): second(u, c1, lambda h, mine, k: Pb[mat_(u), h, mine, k], c2)
+    def S2x(u):
+        @pl.when(mat_(u) == 0)
+        def _(): second(u, c1x, lambda h, mine, k: Pb[mat_(u), h, k, x], c2x)
     def S3(u):
-        for q in c2(u): q.wait()
-        for h in range(TWO):
-            s = Q[par(u), x, h].astype(f32)
-            for d in range(MATS): s = s + R2[ring(u), d, h].astype(f32)
-            U[par(u), h] = s.astype(bf)
+        def go(got, mine):
+            for q in got(u): q.wait()
+            for h in range(TWO): U[par(u), h] = added(Q[par(u), mine[h], h], [R2[deep(u), d, h] for d in range(MATS)])
+        either(u, go, (c2, (x, x)), (c2x, (y, z)))
         start(c3(u, False))
     def S4(u):
         for q in c3(u, False): q.wait_send()
@@ -199,8 +214,12 @@
         start(c4(u))
     def a2a(u, i):
         lay, n = u // OFFLAY, DEV * ((u % OFFLAY) // MATS) + i
-        src, dst = GT.at[u, blk(i, SUB)], gd_o.at[1 - lay, blk(n % NT, SUB), blk(me, LANES)]
-        return n // NT, rd(src, dst, a2s, a2r.at[lay], (0, r_, n // NT)), cpy(src, dst, locsem)
+        to = n // NT
+        src, dst = GT.at[u, blk(i, SUB)], gd_o.at[1 - lay, blk(n - NT * to, SUB), blk(me, LANES)]
+        @pl.when(to != me)
+        def _(): rd(src, dst, a2s, a2r.at[lay], (0, r_, to)).start()
+        @pl.when(to == me)
+        def _(): cpy(src, dst, locsem).start()
     def S5(u):
         for q in c4(u): q.wait()
         v = GT[u].astype(f32)
@@ -209,20 +228,18 @@
         def _(): cpy(GT.at[u], gt_o.at[u], gtsem).start()
         @pl.when(u % MATS == 0)
         def _():
-            def one(i):
-                @pl.when(a2a(u, i)[0] != me)
-                def _(): a2a(u, i)[1].start()
-                @pl.when(a2a(u, i)[0] == me)
-                def _(): a2a(u, i)[TWO].start()
-            each(0, DEV, one)
-    STAGES = (S5, S4, S3, S2, S1)
+            each(0, DEV, lambda i: a2a(u, i))
+    LAST = TWO * len((S1, S2, S3, S4, S5))
+    STAGES = ((S5, LAST), (S4, LAST - TWO), (S3, LAST - RING), (S2, RING), (S2x, NT), (S1, TWO))
     def slot(t):
-        for i, S in enumerate(STAGES):
-            u = t - TWO * (len(STAGES) - i)
-            @pl.when(jnp.logical_and(u >= 0, u < NU))
-            def _(): S(u)
+        for S, lag in STAGES:
+            @pl.when(jnp.logical_and(t >= lag, t < NU + lag))
+            def _(): S(t - lag)
 
     each(0, MATS, A0)
+    for l in range(TWO):
+        wt(staged[l], ownsem.at[l])
+        cpy(staged[l], WD.at[l, blk(me, SH), :], ownsem.at[l]).start()
     wt(ap, psem)
     def xnorm(i):
         wide = ya[1, blk(i, CH), :].astype(f32)
@@ -240,7 +257,7 @@
     gu_load(0, 0, 0)
     each(MATS, RING, A1)
     each(NT, DEEP, A0)
-    def stv(i): return acc.at[blk(i, TF), :]
+    def stv(i): return acc.at[blk(i, TF2), :]
     def step1(j):
         b = par(j)
         gu_wait(b)
@@ -248,23 +265,25 @@
         hr = blk(hs, TF)
         @pl.when(j >= MATS)
         def _(): wt(H.at[cut(TF)], hsem.at[hs])
+        @pl.when(j > 0)
+        def _(): guard(A2, j + 1)
         def sub(s):
-            i = j * RING + s
-            k = i % MATS
-            @pl.when(i >= MATS)
-            def _(): wt(stv(0), stsem.at[k])
-            gu = dot_(wgu[b], ya[1, blk(s, TK), :], 0, 1)
-            g, u = gu[:TF], gu[TF:]
-            sg = jax.nn.sigmoid(g)
-            si = g * sg
-            acc[blk(k, TF), 0:TK] = si
-            acc[blk(k, TF), TK:] = u * (sg + si * (1 - sg))
-            H[hr, blk(s, TK)] = (si * u).astype(bf)
-            cpy(stv(k), AB_h.at[i], stsem.at[k]).start()
+            @pl.when(j > 0)
+            def _(): wt(stv(0), stsem.at[s])
+            for q in range(NCH):
+                t, cols = pl.ds(pl.multiple_of(s * TB + q * TC, TC), TC), pl.ds(q * TC, TC)
+                gu = dot_(wgu[b], ya[1, t, :], 0, 1)
+                g, u = gu[:TF], gu[TF:]
+                sg = jax.nn.sigmoid(g)
+                si = g * sg
+                acc[pl.ds(mul(s, TF2), TF), cols] = si
+                acc[pl.ds(pl.multiple_of(s * TF2 + TF, TF), TF), cols] = u * (sg + si * (1 - sg))
+                H[hr, t] = (si * u).astype(bf)
+            cpy(stv(s), AB_h.at[TWO * j + s], stsem.at[s]).start()
             @pl.when(s == 0)
-            def _(): guard(A2, j + 1)
-            @pl.when(s == TWO)
             def _():
+                @pl.when(j == 0)
+                def _(): A2(j + 1)
                 guard(A3, j + 1)
                 @pl.when(j < NT - 1)
                 def _(): gu_load(0, j + 1, 1 - b)
@@ -272,15 +291,15 @@
                 def _(): cpy(WD.at[0, pl.ds(TF3, TF2), :], wdb, wdsem.at[TWO]).start()
                 guard(A1, j + RING)
                 guard(A0, j + DEEP)
-        each(0, RING, sub)
+        each(0, TWO, sub)
         cpy(H.at[hr], h_h.at[blk(j, TF), :], hsem.at[hs]).start()
     each(0, NT, step1)
-    for i in range(MATS): wt(stv(0), stsem.at[i])
+    for i in range(TWO): wt(stv(0), stsem.at[i])
     wt(ap, asem)
     start(permuted(x_h, ap, psem))
     lo, mid = cut(TF2), wgu.at[0, cut(TF), cut(D)]
     cpy(WD.at[0, pl.ds(TF2, TF), :], mid, wdsem.at[0]).start()
-    acc[...] = jnp.zeros_like(acc)
+    acc[0:T, :] = jnp.zeros((T, D), f32)
     def down(i):
         @pl.when(i == 1)
         def _(): wt(H.at[lo], hsem.at[MATS])
@@ -327,22 +346,23 @@
     wt(dyp, dysem)
 
     def h1l(k): return cpy(h1p_h.at[pl.ds(k * D, D)], H.at[cut(D), pl.ds(k * D, D)], hsem.at[k])
-    def abl(i): return cpy(AB_h.at[i], stv(i % MATS), stsem.at[i % MATS])
+    def abl(j, s): return cpy(AB_h.at[TWO * j + s], stv(s), stsem.at[s])
     def hload(j): return cpy(h_h.at[blk(j, TF), :], H.at[cut(TF)], hsem.at[TWO])
     def layer1(k, b):
         gu_wait(b)
         @pl.when(k + 1 < NT)
         def _(): gu_load(1, k + 1, 1 - b)
         def half(h):
-            t = blk(h, TB)
-            gu = dot_(wgu[b], ya[1, t, :], 0, 1)
-            g, u = gu[:TF], gu[TF:]
-            dh = dot_(wdb[blk(par(k), TF)], ya[0, t, :], 1, 1).astype(bf).astype(f32)
-            sg = jax.nn.sigmoid(g)
-            si = g * sg
-            H[0:TF, t] = (si * u).astype(bf)
-            H[TF2:TF3, t] = (dh * si).astype(bf)
-            H[TF:TF2, t] = (dh * u * (sg + si * (1 - sg))).astype(bf)
+            for q in range(NCH):
+                t = pl.ds(pl.multiple_of(h * TB + q * TC, TC), TC)
+                gu = dot_(wgu[b], ya[1, t, :], 0, 1)
+                g, u = gu[:TF], gu[TF:]
+                dh = dot_(wdb[blk(par(k), TF)], ya[0, t, :], 1, 1).astype(bf).astype(f32)
+                sg = jax.nn.sigmoid(g)
+                si = g * sg
+                H[0:TF, t] = (si * u).astype(bf)
+                H[TF2:TF3, t] = (dh * si).astype(bf)
+                H[TF:TF2, t] = (dh * u * (sg + si * (1 - sg))).astype(bf)
             @pl.when(h == 0)
             def _(): guard(A2, k + DEEP + MATS)
         each(0, TWO, half)
@@ -358,21 +378,23 @@
             inner = jnp.mean(da * wide, -1, keepdims=True)
             dw = (da * scale - wide * (scale * scale * scale * inner)).astype(bf)
             ya[0, r, :] = (ya[0, r, :].astype(f32) + dw.astype(f32)).astype(bf)
+            @pl.when(i == TF2 // CH - 1)
+            def _(): abl(0, 0).start()
         each(0, T // CH, nb)
-        for i in range(TWO): abl(i).start()
+        abl(0, 1).start()
         hload(0).start()
         wt(ap, asem)
     def layer0(j, b):
         def sub(s):
-            i = j * RING + s
-            @pl.when(i + TWO < NT * RING)
-            def _(): abl(i + TWO).start()
-            abl(i).wait()
-            t, r = blk(s, TK), blk(i % MATS, TF)
-            dh = dot_(wdb[blk(b, TF)], ya[0, t, :], 1, 1).astype(bf).astype(f32)
-            H[TF2:TF3, t] = (dh * acc[r, 0:TK]).astype(bf)
-            H[TF:TF2, t] = (dh * acc[r, TK:]).astype(bf)
-        each(0, RING, sub)
+            abl(j, s).wait()
+            for q in range(NCH):
+                t, cols = pl.ds(pl.multiple_of(s * TB + q * TC, TC), TC), pl.ds(q * TC, TC)
+                dh = dot_(wdb[blk(b, TF)], ya[0, t, :], 1, 1).astype(bf).astype(f32)
+                H[TF2:TF3, t] = (dh * acc[pl.ds(mul(s, TF2), TF), cols]).astype(bf)
+                H[TF:TF2, t] = (dh * acc[pl.ds(pl.multiple_of(s * TF2 + TF, TF), TF), cols]).astype(bf)
+            @pl.when(j + 1 < NT)
+            def _(): abl(j + 1, s).start()
+        each(0, TWO, sub)
         hload(j).wait()
     def tile(k):
         b, gb = par(k), par(k + 1)
@@ -401,7 +423,7 @@
             def _(): hload(k - NT + 1).start()
         each(0, MATS, mat)
     each(0, TWO * NT, tile)
-    each(NU, NU + TWO * len(STAGES), slot)
+    each(NU, NU + LAST, slot)
 
     SQ[me] = sqa[...]
     def sqc(e, i): return rd(sqa, SQ.at[i], sqs.at[e - 1], sqr.at[i], (0, r_, (me + e) % DEV))
@@ -426,18 +448,18 @@
     p3, r3, d3 = (TWO, TWO, MATS), (RING, TWO, MATS), (DEEP, TWO, MATS)
     one, two, three = S, S((TWO,)), S((MATS,))
     outs = [sds((NU, TF, LANES), bf), sds((TWO, SH, D), bf), sds((DEV, LANES), f32), sds((TWO, DEV, TWO, LANES, F), bf), sds((TWO, F, D), bf),
-            sds((T, D), bf), sds((T, D), bf), sds((NT * RING, TF, D), f32), sds((F, T), bf)]
+            sds((T, D), bf), sds((T, D), bf), sds((NT * TWO, TF2, D), f32), sds((F, T), bf)]
     specs = [hbm] * len(outs)
     specs[TWO] = pl.BlockSpec(memory_space=pltpu.VMEM)
     return pl.pallas_call(
         step_kernel,
         out_shape=outs, in_specs=[hbm] * (MATS + TWO), out_specs=specs,
         scratch_shapes=[
-            V((TWO, T, D), bf), V((T, D), f32), V((TWO, D, TF2), bf), V((TF2, D), bf), V((TF3, T), bf), V((TWO, TF, D), bf), V((RING, TF, HALF), bf),
-            V((TWO, TWO, RING, RING) + b, bf), V(r3 + (RING,) + b, bf), V((TWO, RING, TWO) + b, bf), V((RING, MATS, TWO) + b, bf), V((TWO, TWO) + b, bf), V((RING, TWO, RING) + b, bf),
+            V((TWO, T, D), bf), V((TWO * TF2, D), f32), V((TWO, D, TF2), bf), V((TF2, D), bf), V((TF3, T), bf), V((TWO, TF, D), bf), V((RING, TF, HALF), bf),
+            V((MATS, TWO, RING, RING) + b, bf), V(r3 + (RING,) + b, bf), V((TWO, RING, TWO) + b, bf), V((DEEP, MATS, TWO) + b, bf), V((TWO, TWO) + b, bf), V((RING, TWO, RING) + b, bf),
             V((NU, TF, LANES), bf), V((DEV, LANES), f32), V((DEV, DEV, LANES), f32),
-            one, one, one, two, two, three, three, S((RING,)), one, one,
-            two, S((RING,)), S(p3), S(r3), S((TWO, MATS)), S((RING, MATS)), S(p3), S((RING, TWO, RING)), S(p3), S(r3), one, two,
+            one, one, one, two, two, three, two, S((RING,)), one, one,
+            two, S((RING,)), S(r3), S(r3), S(p3), S(d3), S(p3), S((RING, TWO, RING)), S(p3), S(r3), one, two,
             S(d3), S(d3), S((NA,)), S((NA,)), S(d3), S(d3), S((DEEP,)), S((NA,)), S((DEV - 1,)), S((DEV,))],
         compiler_params=pltpu.CompilerParams(collective_id=0, has_side_effects=True, vmem_limit_bytes=VMEM_LIMIT),
         name="train")(x, dy, wg, wu, wd)

time: 373 us -> 371 us (level)
  no operation moved by 1% of the time
where the time goes in v2:
time: 371 us; the launch traced here: 370 us
  Pallas kernels  370 us (100%)
    pallas_call x1, Pallas kernels, train(): pl.pallas_call(step_kernel, out_shape=outs, in_specs=[hbm] * (MATS + TWO)...  349 us
    pallas_call x1, Pallas kernels, optimizer(): pl.pallas_call(kernel, grid=(TWO, NT), in_specs=[pl.BlockSpec((DEV, LANES...  20.2 us

profile of v2, /device:TPU:1, one launch (start us, length us, event | category | flops | bytes accessed | tf_op | source)
XLA Modules:
  0.0 370.4 jit_solution(18200081970128169518)
XLA Ops:
  0.6 349.4 %train.1 = (bf16[30,640,128]{2,1,0:T(8,128)(2,1)}, bf16[2,400,1024]{2,1,0:T(8,128)(2,1)}, f32[8,128]{1,0:T(8,128)}, bf16[2,8,2,128,3200]{4,3,2,1,0:T(8,128)(2,1)...) custom-call(bf16[2048,1024]{1,0:T(8,128)(2,1)} %bitcast.2, ...), custom_call_target="tpu_custom_call" | custom-call | tf_op jit(solution)/shard_map/train/pallas_call | solution.py:454
  350.0 20.2 %optimizer.1 = (bf16[2,128,3200]{2,1,0:T(8,128)(2,1)}, bf16[2,128,3200]{2,1,0:T(8,128)(2,1)}, bf16[2,400,1024]{2,1,0:T(8,128)(2,1)}, f32[2,128,3200]{2,1,0:T(8,1...) custom-call(f32[8,128]{1,0:T(8,128)} %get-tuple-element.12.sq, ...), custom_call_target="tpu_custom_call" | custom-call | tf_op jit(solution)/shard_map/optimizer/pallas_call | solution.py:484

commit v3 on v2

--- a/solution.py
+++ b/solution.py
@@ -92,40 +92,37 @@
         def _(): fg(u // (NT + TWO), u % (NT + TWO))
         @pl.when(u % (NT + TWO) >= NT)
         def _(): fd(u - NT)
-    def wait6(ref, ss, rs, b):
-        def one(i):
-            h, d = i // MATS, i % MATS
-            wt(ref, ss.at[b, h, d])
-            wt(ref, rs.at[b, h, d])
-        each(0, DEEP, one)
+    def both(ref, ss, rs, b):
+        wt(ref, ss.at[b])
+        wt(ref, rs.at[b])
     def A0(u):
         b = u % DEEP
         def fg(l, j):
             for m, inp in enumerate((wg_i, wu_i)):
                 def one(i):
-                    for h, q, _ in AX: rd(inp.at[l, q16(h, q), blk(j, TF)], WGU.at[l, own, m, q16(h, q), blk(j, TF)], ag0s.at[b, h, i], ag0r.at[b, h, i], xdev(i + 1)).start()
+                    for h, q, _ in AX: rd(inp.at[l, q16(h, q), blk(j, TF)], WGU.at[l, own, m, q16(h, q), blk(j, TF)], ag0s.at[b], ag0r.at[b], xdev(i + 1)).start()
                 each(0, MATS, one)
                 rd(inp.at[l, :, blk(j, TF)], WGU.at[l, own, m, :, blk(j, TF)], agds.at[u], agdr.at[u], part).start()
         def fd(l):
             wt(WD.at[0, cut(SH), :], ownsem.at[l])
             def one(i):
-                for h, q, _ in AX: same(WD.at[l, blk(me, SH), colq(h, q)], ag0s.at[b, h, i], ag0r.at[b, h, i], xdev(i + 1)).start()
+                for h, q, _ in AX: same(WD.at[l, blk(me, SH), colq(h, q)], ag0s.at[b], ag0r.at[b], xdev(i + 1)).start()
             each(0, MATS, one)
             same(WD.at[l, blk(me, SH), :], agds.at[u], agdr.at[u], part).start()
         fork(u, fg, fd)
     def A1(u):
         b = u % DEEP
         def fg(l, j):
-            wait6(WGU.at[0, 0, :, cut(AROWS), cut(TF)], ag0s, ag0r, b)
+            both(WGU.at[0, cut(DEEP), :, cut(AROWS), cut(TF)], ag0s, ag0r, b)
             def one(i):
                 k, d = c * RING + ring(x + i // MATS + 1), i % MATS
-                for h, q, f in AX: same(WGU.at[l, k, :, q16(h, q), blk(j, TF)], ag1s.at[b, h, d], ag1r.at[b, h, d], f(d + 1)).start()
+                for h, q, f in AX: same(WGU.at[l, k, :, q16(h, q), blk(j, TF)], ag1s.at[b], ag1r.at[b], f(d + 1)).start()
             each(0, MATS * MATS, one)
         def fd(l):
-            wait6(WD.at[0, cut(SH), cut(LANES)], ag0s, ag0r, b)
+            both(WD.at[0, cut(DEEP * SH), cut(LANES)], ag0s, ag0r, b)
             def one(i):
                 k, d = TWO * ring(x + i // MATS + 1) + c, i % MATS
-                for h, q, f in AX: same(WD.at[l, blk(k, SH), colq(h, q)], ag1s.at[b, h, d], ag1r.at[b, h, d], f(d + 1)).start()
+                for h, q, f in AX: same(WD.at[l, blk(k, SH), colq(h, q)], ag1s.at[b], ag1r.at[b], f(d + 1)).start()
             each(0, MATS * MATS, one)
         fork(u, fg, fd)
     gu1, gu3 = WGU.at[0, 0, :, :, cut(TF)], WGU.at[0, cut(MATS), :, :, cut(TF)]
@@ -133,10 +130,10 @@
     def A2(u):
         b = u % DEEP
         def fg(l, j):
-            wait6(WGU.at[0, cut(MATS), :, cut(AROWS), cut(TF)], ag1s, ag1r, b)
+            both(WGU.at[0, cut(DEEP), :, cut(MATS * AROWS), cut(TF)], ag1s, ag1r, b)
             each(1, RING, lambda i: same(WGU.at[l, c * RING + ring(x + i), :, :, blk(j, TF)], ag2s.at[b], ag2r.at[u], part).start())
         def fd(l):
-            wait6(WD.at[0, cut(MATS * SH), cut(LANES)], ag1s, ag1r, b)
+            both(WD.at[0, cut(DEEP * SH), cut(MATS * LANES)], ag1s, ag1r, b)
             each(1, RING, lambda i: same(WD.at[l, blk(TWO * ring(x + i) + c, SH), :], ag2s.at[b], ag2r.at[u], part).start())
         fork(u, fg, fd)
     def A3(u):
@@ -152,59 +149,55 @@
     def mat_(u): return u % MATS
     def deep(u): return u % DEEP
     def c1(u):
-        return [rd(Pb.at[mat_(u), h, ring(q + d)], R1.at[ring(u), h, d - 1], s1s.at[ring(u), h, d - 1], s1r.at[ring(u), h, d - 1], f(d)) for d in OFFS for h, q, f in AX]
-    def c1x(u): return [rd(Pb.at[mat_(u), :, :, ring(x + d)], R1.at[ring(u), :, d - 1], s1s.at[ring(u), 0, d - 1], s1r.at[ring(u), 0, d - 1], xdev(d)) for d in OFFS]
-    def c2(u): return [rd(Q.at[par(u), ring(x + d)], R2.at[deep(u), d - 1], s2s.at[par(u), 0, d - 1], s2r.at[deep(u), 0, d - 1], xdev(d)) for d in OFFS]
+        return [rd(Pb.at[mat_(u), h, ring(q + d)], R1.at[ring(u), h, d - 1], s1s.at[ring(u)], s1r.at[ring(u)], f(d)) for d in OFFS for h, q, f in AX]
+    def c1x(u): return [rd(Pb.at[mat_(u), :, :, ring(x + d)], R1.at[ring(u), :, d - 1], s1s.at[ring(u)], s1r.at[ring(u)], xdev(d)) for d in OFFS]
+    def c2(u): return [rd(Q.at[par(u), ring(x + d)], R2.at[deep(u), d - 1], s2s.at[par(u)], s2r.at[deep(u)], xdev(d)) for d in OFFS]
     def c2x(u):
-        return [rd(Q.at[par(u), ring(q + d), h], R2.at[deep(u), d - 1, h], s2s.at[par(u), h, d - 1], s2r.at[deep(u), h, d - 1], f(d)) for d in OFFS for h, q, f in AX]
+        return [rd(Q.at[par(u), ring(q + d), h], R2.at[deep(u), d - 1, h], s2s.at[par(u)], s2r.at[deep(u)], f(d)) for d in OFFS for h, q, f in AX]
     def either(u, f, *args):
         @pl.when(mat_(u) > 0)
         def _(): f(*args[0])
         @pl.when(mat_(u) == 0)
         def _(): f(*args[1])
-    def c3(u, recv):
-        o = []
-        for d in OFFS:
-            for h, q, f in ((0, z, zdev), (1, y, ydev)):
-                k = ring(q + d) if recv else q
-                o.append(rd(U.at[par(u), h], R3.at[ring(u), h, k], s3s.at[par(u), h, d - 1], s3r.at[ring(u), h, k], f(d)))
-        return o
+    def c3(u):
+        return [rd(U.at[par(u), h], R3.at[ring(u), h, q], s3s.at[par(u)], s3r.at[ring(u)], f(d)) for d in OFFS for h, q, f in ((0, z, zdev), (1, y, ydev))]
     def rows(h, q): return pl.ds(pl.multiple_of(h * (TF // TWO) + q * SUB, SUB), SUB)
     def c4(u):
-        return [same(GT.at[u, rows(h, q)], s4s.at[par(u), h, d - 1], s4r.at[ring(u), h, d - 1], f(d)) for d in OFFS for h, q, f in AX]
+        return [same(GT.at[u, rows(h, q)], s4s.at[par(u)], s4r.at[ring(u)], f(d)) for d in OFFS for h, q, f in AX]
     def S0(u): c0(u).start()
     def S1(u):
         c0(u).wait()
-        def one(i):
+        for i in range(DEV):
             for k in range(RING):
-                mine = G[par(u), blk(i, SUB), blk(c * RING + k, LANES)]
-                Pb[mat_(u), i // RING, ring(i), k] = (mine.astype(f32) + R0[ring(u), blk(i, SUB), pl.ds(k * LANES, LANES)].astype(f32)).astype(bf)
-        each(0, DEV, one)
+                mine = G[par(u), pl.ds(i * SUB, SUB), blk(c * RING + k, LANES)]
+                Pb[mat_(u), i // RING, i % RING, k] = (mine.astype(f32) + R0[ring(u), pl.ds(i * SUB, SUB), pl.ds(k * LANES, LANES)].astype(f32)).astype(bf)
         either(u, lambda way: start(way(u)), (c1,), (c1x,))
     def added(first, rest):
         s = first.astype(f32)
         for q in rest: s = s + q.astype(f32)
         return s.astype(bf)
-    def second(u, got, first, send):
-        for q in got(u): q.wait()
+    def second(u, first, send):
+        wt(R1.at[0], s1s.at[ring(u)])
+        wt(R1.at[0], s1r.at[ring(u)])
         for h, mine, _ in AX:
             for k in range(RING): Q[par(u), k, h] = added(first(h, mine, k), [R1[ring(u), h, d, k] for d in range(MATS)])
         start(send(u))
     def S2(u):
         @pl.when(mat_(u) > 0)
-        def _(): second(u, c1, lambda h, mine, k: Pb[mat_(u), h, mine, k], c2)
+        def _(): second(u, lambda h, mine, k: Pb[mat_(u), h, mine, k], c2)
     def S2x(u):
         @pl.when(mat_(u) == 0)
-        def _(): second(u, c1x, lambda h, mine, k: Pb[mat_(u), h, k, x], c2x)
+        def _(): second(u, lambda h, mine, k: Pb[mat_(u), h, k, x], c2x)
     def S3(u):
-        def go(got, mine):
-            for q in got(u): q.wait()
+        wt(R2.at[0], s2s.at[par(u)])
+        wt(R2.at[0], s2r.at[deep(u)])
+        def go(*mine):
             for h in range(TWO): U[par(u), h] = added(Q[par(u), mine[h], h], [R2[deep(u), d, h] for d in range(MATS)])
-        either(u, go, (c2, (x, x)), (c2x, (y, z)))
-        start(c3(u, False))
+        either(u, go, (x, x), (y, z))
+        start(c3(u))
     def S4(u):
-        for q in c3(u, False): q.wait_send()
-        for q in c3(u, True): q.wait_recv()
+        wt(R2.at[0], s3s.at[par(u)])
+        wt(R2.at[0], s3r.at[ring(u)])
         R3[ring(u), 0, z] = U[par(u), 0]
         R3[ring(u), 1, y] = U[par(u), 1]
         for h, q, _ in AX:
@@ -221,7 +214,8 @@
         @pl.when(to == me)
         def _(): cpy(src, dst, locsem).start()
     def S5(u):
-        for q in c4(u): q.wait()
+        wt(R2.at[0], s4s.at[par(u)])
+        wt(R2.at[0], s4r.at[ring(u)])
         v = GT[u].astype(f32)
         sqa[...] += jnp.sum((v * v).reshape(SUB, DEV, LANES), axis=0)
         @pl.when(u % MATS > 0)
@@ -426,16 +420,14 @@
     each(NU, NU + LAST, slot)
 
     SQ[me] = sqa[...]
-    def sqc(e, i): return rd(sqa, SQ.at[i], sqs.at[e - 1], sqr.at[i], (0, r_, (me + e) % DEV))
+    def sqc(e, i): return rd(sqa, SQ.at[i], sqs, sqr, (0, r_, (me + e) % DEV))
     for e in range(1, DEV): sqc(e, me).start()
     def drain(n, k, sem): wt(GT.at[cut(n), cut(k)], sem)
     drain(NU - TWO * NT, TF, gtsem)
     drain(TWO, SH, locsem)
     drain(TWO * (DEV - 1), SH, a2s)
     for l in range(TWO): drain(DEV - 1, SH, a2r.at[l])
-    for e in range(1, DEV):
-        sqc(e, me).wait_send()
-        sqc(e, (me + e) % DEV).wait_recv()
+    for sem in (sqs, sqr): wt(SQ.at[cut(DEV - 1)], sem)
     tot = SQ[0]
     for i in range(1, DEV): tot = tot + SQ[i]
     sq_o[...] = tot
@@ -445,8 +437,8 @@
     hbm = pl.BlockSpec(memory_space=pl.ANY)
     V, S = pltpu.VMEM, pltpu.SemaphoreType.DMA
     b = (SUB, LANES)
-    p3, r3, d3 = (TWO, TWO, MATS), (RING, TWO, MATS), (DEEP, TWO, MATS)
-    one, two, three = S, S((TWO,)), S((MATS,))
+    r3 = (RING, TWO, MATS)
+    one, two, three, four, six = S, S((TWO,)), S((MATS,)), S((RING,)), S((DEEP,))
     outs = [sds((NU, TF, LANES), bf), sds((TWO, SH, D), bf), sds((DEV, LANES), f32), sds((TWO, DEV, TWO, LANES, F), bf), sds((TWO, F, D), bf),
             sds((T, D), bf), sds((T, D), bf), sds((NT * TWO, TF2, D), f32), sds((F, T), bf)]
     specs = [hbm] * len(outs)
@@ -459,8 +451,8 @@
             V((MATS, TWO, RING, RING) + b, bf), V(r3 + (RING,) + b, bf), V((TWO, RING, TWO) + b, bf), V((DEEP, MATS, TWO) + b, bf), V((TWO, TWO) + b, bf), V((RING, TWO, RING) + b, bf),
             V((NU, TF, LANES), bf), V((DEV, LANES), f32), V((DEV, DEV, LANES), f32),
             one, one, one, two, two, three, two, S((RING,)), one, one,
-            two, S((RING,)), S(r3), S(r3), S(p3), S(d3), S(p3), S((RING, TWO, RING)), S(p3), S(r3), one, two,
-            S(d3), S(d3), S((NA,)), S((NA,)), S(d3), S(d3), S((DEEP,)), S((NA,)), S((DEV - 1,)), S((DEV,))],
+            two, four, four, four, two, six, two, four, two, four, one, two,
+            six, six, S((NA,)), S((NA,)), six, six, six, S((NA,)), one, one],
         compiler_params=pltpu.CompilerParams(collective_id=0, has_side_effects=True, vmem_limit_bytes=VMEM_LIMIT),
         name="train")(x, dy, wg, wu, wd)
 

time: 371 us -> 363 us (0.978)
  Pallas kernels: 370 us -> 362 us
    pallas_call x1, Pallas kernels: 349 us -> 342 us  [train(): pl.pallas_call(step_kernel, out_shape=outs, in_specs=[hbm] * (MATS + TWO)...]
where the time goes in v3:
time: 363 us
  Pallas kernels  362 us (100%)
    pallas_call x1, Pallas kernels, train(): pl.pallas_call(step_kernel, out_shape=outs, in_specs=[hbm] * (MATS + TWO)...  342 us
    pallas_call x1, Pallas kernels, optimizer(): pl.pallas_call(kernel, grid=(TWO, NT), in_specs=[pl.BlockSpec((DEV, LANES...  20.2 us

profile of v3, /device:TPU:1, one launch (start us, length us, event | category | flops | bytes accessed | tf_op | source)
XLA Modules:
  0.0 362.9 jit_solution(16309951042503024749)
XLA Ops:
  0.6 341.9 %train.1 = (bf16[30,640,128]{2,1,0:T(8,128)(2,1)}, bf16[2,400,1024]{2,1,0:T(8,128)(2,1)}, f32[8,128]{1,0:T(8,128)}, bf16[2,8,2,128,3200]{4,3,2,1,0:T(8,128)(2,1)...) custom-call(bf16[2048,1024]{1,0:T(8,128)(2,1)} %bitcast.2, ...), custom_call_target="tpu_custom_call" | custom-call | tf_op jit(solution)/shard_map/train/pallas_call | solution.py:446
  342.5 20.2 %optimizer.1 = (bf16[2,128,3200]{2,1,0:T(8,128)(2,1)}, bf16[2,128,3200]{2,1,0:T(8,128)(2,1)}, bf16[2,400,1024]{2,1,0:T(8,128)(2,1)}, f32[2,128,3200]{2,1,0:T(8,1...) custom-call(f32[8,128]{1,0:T(8,128)} %get-tuple-element.12.sq, ...), custom_call_target="tpu_custom_call" | custom-call | tf_op jit(solution)/shard_map/optimizer/pallas_call | solution.py:476

commit v4 on v3

--- a/solution.py
+++ b/solution.py
@@ -151,19 +151,19 @@
     def c1(u):
         return [rd(Pb.at[mat_(u), h, ring(q + d)], R1.at[ring(u), h, d - 1], s1s.at[ring(u)], s1r.at[ring(u)], f(d)) for d in OFFS for h, q, f in AX]
     def c1x(u): return [rd(Pb.at[mat_(u), :, :, ring(x + d)], R1.at[ring(u), :, d - 1], s1s.at[ring(u)], s1r.at[ring(u)], xdev(d)) for d in OFFS]
-    def c2(u): return [rd(Q.at[par(u), ring(x + d)], R2.at[deep(u), d - 1], s2s.at[par(u)], s2r.at[deep(u)], xdev(d)) for d in OFFS]
+    def c2(u): return [rd(Q.at[ring(u), ring(x + d)], R2.at[deep(u), d - 1], s2s.at[ring(u)], s2r.at[deep(u)], xdev(d)) for d in OFFS]
     def c2x(u):
-        return [rd(Q.at[par(u), ring(q + d), h], R2.at[deep(u), d - 1, h], s2s.at[par(u)], s2r.at[deep(u)], f(d)) for d in OFFS for h, q, f in AX]
+        return [rd(Q.at[ring(u), ring(q + d), h], R2.at[deep(u), d - 1, h], s2s.at[ring(u)], s2r.at[deep(u)], f(d)) for d in OFFS for h, q, f in AX]
     def either(u, f, *args):
         @pl.when(mat_(u) > 0)
         def _(): f(*args[0])
         @pl.when(mat_(u) == 0)
         def _(): f(*args[1])
     def c3(u):
-        return [rd(U.at[par(u), h], R3.at[ring(u), h, q], s3s.at[par(u)], s3r.at[ring(u)], f(d)) for d in OFFS for h, q, f in ((0, z, zdev), (1, y, ydev))]
+        return [rd(U.at[ring(u), h], R3.at[deep(u), h, q], s3s.at[ring(u)], s3r.at[deep(u)], f(d)) for d in OFFS for h, q, f in ((0, z, zdev), (1, y, ydev))]
     def rows(h, q): return pl.ds(pl.multiple_of(h * (TF // TWO) + q * SUB, SUB), SUB)
     def c4(u):
-        return [same(GT.at[u, rows(h, q)], s4s.at[par(u)], s4r.at[ring(u)], f(d)) for d in OFFS for h, q, f in AX]
+        return [same(GT.at[u, rows(h, q)], s4s.at[ring(u)], s4r.at[deep(u)], f(d)) for d in OFFS for h, q, f in AX]
     def S0(u): c0(u).start()
     def S1(u):
         c0(u).wait()
@@ -180,7 +180,7 @@
         wt(R1.at[0], s1s.at[ring(u)])
         wt(R1.at[0], s1r.at[ring(u)])
         for h, mine, _ in AX:
-            for k in range(RING): Q[par(u), k, h] = added(first(h, mine, k), [R1[ring(u), h, d, k] for d in range(MATS)])
+            for k in range(RING): Q[ring(u), k, h] = added(first(h, mine, k), [R1[ring(u), h, d, k] for d in range(MATS)])
         start(send(u))
     def S2(u):
         @pl.when(mat_(u) > 0)
@@ -189,20 +189,20 @@
         @pl.when(mat_(u) == 0)
         def _(): second(u, lambda h, mine, k: Pb[mat_(u), h, k, x], c2x)
     def S3(u):
-        wt(R2.at[0], s2s.at[par(u)])
+        wt(R2.at[0], s2s.at[ring(u)])
         wt(R2.at[0], s2r.at[deep(u)])
         def go(*mine):
-            for h in range(TWO): U[par(u), h] = added(Q[par(u), mine[h], h], [R2[deep(u), d, h] for d in range(MATS)])
+            for h in range(TWO): U[ring(u), h] = added(Q[ring(u), mine[h], h], [R2[deep(u), d, h] for d in range(MATS)])
         either(u, go, (x, x), (y, z))
         start(c3(u))
     def S4(u):
-        wt(R2.at[0], s3s.at[par(u)])
-        wt(R2.at[0], s3r.at[ring(u)])
-        R3[ring(u), 0, z] = U[par(u), 0]
-        R3[ring(u), 1, y] = U[par(u), 1]
+        wt(R2.at[0], s3s.at[ring(u)])
+        wt(R2.at[0], s3r.at[deep(u)])
+        R3[deep(u), 0, z] = U[ring(u), 0]
+        R3[deep(u), 1, y] = U[ring(u), 1]
         for h, q, _ in AX:
-            s = R3[ring(u), h, 0].astype(f32)
-            for d in OFFS: s = s + R3[ring(u), h, d].astype(f32)
+            s = R3[deep(u), h, 0].astype(f32)
+            for d in OFFS: s = s + R3[deep(u), h, d].astype(f32)
             GT[u, rows(h, q)] = s.astype(bf)
         start(c4(u))
     def a2a(u, i):
@@ -214,8 +214,8 @@
         @pl.when(to == me)
         def _(): cpy(src, dst, locsem).start()
     def S5(u):
-        wt(R2.at[0], s4s.at[par(u)])
-        wt(R2.at[0], s4r.at[ring(u)])
+        wt(R2.at[0], s4s.at[ring(u)])
+        wt(R2.at[0], s4r.at[deep(u)])
         v = GT[u].astype(f32)
         sqa[...] += jnp.sum((v * v).reshape(SUB, DEV, LANES), axis=0)
         @pl.when(u % MATS > 0)
@@ -224,11 +224,14 @@
         def _():
             each(0, DEV, lambda i: a2a(u, i))
     LAST = TWO * len((S1, S2, S3, S4, S5))
-    STAGES = ((S5, LAST), (S4, LAST - TWO), (S3, LAST - RING), (S2, RING), (S2x, NT), (S1, TWO))
+    STAGES = ((S2, RING, NU), (S2x, NT, NU), (S3, LAST - RING, NU), (S1, TWO, NU - 1), (S4, LAST - TWO, NU), (S5, LAST, NU))
     def slot(t):
-        for S, lag in STAGES:
-            @pl.when(jnp.logical_and(t >= lag, t < NU + lag))
+        for S, lag, end in STAGES:
+            @pl.when(jnp.logical_and(t >= lag, t < end + lag))
             def _(): S(t - lag)
+            if S is S1:
+                @pl.when(t == NU)
+                def _(): S1(t - 1)
 
     each(0, MATS, A0)
     for l in range(TWO):
@@ -293,12 +296,16 @@
     start(permuted(x_h, ap, psem))
     lo, mid = cut(TF2), wgu.at[0, cut(TF), cut(D)]
     cpy(WD.at[0, pl.ds(TF2, TF), :], mid, wdsem.at[0]).start()
-    acc[0:T, :] = jnp.zeros((T, D), f32)
     def down(i):
         @pl.when(i == 1)
         def _(): wt(H.at[lo], hsem.at[MATS])
         wt(wdb, wdsem.at[TWO])
-        def halves(h): acc[blk(h, TB), :] += dot_(H[lo, blk(h, TB)], wdb[...], 0, 0)
+        def halves(h):
+            term = lambda: dot_(H[lo, blk(h, TB)], wdb[...], 0, 0)
+            @pl.when(i == 0)
+            def _(): acc[blk(h, TB), :] = term()
+            @pl.when(i > 0)
+            def _(): acc[blk(h, TB), :] += term()
         each(0, TWO, halves)
         @pl.when(i == 0)
         def _():
@@ -448,36 +455,52 @@
         out_shape=outs, in_specs=[hbm] * (MATS + TWO), out_specs=specs,
         scratch_shapes=[
             V((TWO, T, D), bf), V((TWO * TF2, D), f32), V((TWO, D, TF2), bf), V((TF2, D), bf), V((TF3, T), bf), V((TWO, TF, D), bf), V((RING, TF, HALF), bf),
-            V((MATS, TWO, RING, RING) + b, bf), V(r3 + (RING,) + b, bf), V((TWO, RING, TWO) + b, bf), V((DEEP, MATS, TWO) + b, bf), V((TWO, TWO) + b, bf), V((RING, TWO, RING) + b, bf),
+            V((MATS, TWO, RING, RING) + b, bf), V(r3 + (RING,) + b, bf), V((RING, RING, TWO) + b, bf), V((DEEP, MATS, TWO) + b, bf), V((RING, TWO) + b, bf), V((DEEP, TWO, RING) + b, bf),
             V((NU, TF, LANES), bf), V((DEV, LANES), f32), V((DEV, DEV, LANES), f32),
             one, one, one, two, two, three, two, S((RING,)), one, one,
-            two, four, four, four, two, six, two, four, two, four, one, two,
+            two, four, four, four, four, six, four, six, four, six, one, two,
             six, six, S((NA,)), S((NA,)), six, six, six, S((NA,)), one, one],
         compiler_params=pltpu.CompilerParams(collective_id=0, has_side_effects=True, vmem_limit_bytes=VMEM_LIMIT),
         name="train")(x, dy, wg, wu, wd)
 
 
 def optimizer(sq, GT, GD, w, m, v):
-    def kernel(sq, gg, gu, gd, *r):
+    groups = [(l, i) for l in range(TWO) for i in range(MATS)]
+    def kernel(sq, GT, GD, *r):
+        take = lambda k: r[k * MATS:(k + 1) * MATS]
+        srcs, dsts, bufs = [take(k) for k in range(MATS)], [take(k) for k in range(MATS, DEEP)], [take(k) for k in range(DEEP, DEEP + MATS)]
+        gb, gdb, isem, osem, gsem = r[MATS * (DEEP + MATS):]
+        for l, i in groups:
+            for k in range(MATS): cpy(srcs[k][i].at[l], bufs[k][i].at[l], isem.at[k, l, i]).start()
+            if i == TWO: cpy(GD.at[l], gdb.at[l], gsem.at[l, i]).start()
+            else: start([cpy(GT.at[(1 - l) * OFFLAY + MATS * j + i + 1], gb.at[l, i, j], gsem.at[l, i]) for j in range(NT)])
         tot = jnp.sum(jnp.sum(sq[...], axis=0, keepdims=True), axis=1, keepdims=True)
         factor = jnp.minimum(1.0, 0.5 * lax.rsqrt(tot / (TWO * MATS * D * F) + 1e-30))
-        ws, ms, vs, wo, mo, vo = (r[i * MATS:(i + 1) * MATS] for i in range(TWO * MATS))
-        for i, block in enumerate((gg, gu, gd)):
-            g = block[0].astype(f32)
-            g = (g if i == TWO else g.T) * factor
-            mm = 0.9 * ms[i][0] + 0.1 * g
-            vv = 0.95 * vs[i][0] + 0.05 * g * g
-            ww = ws[i][0].astype(f32)
-            wo[i][0] = (ww - 0.02 * (mm * lax.rsqrt(vv + 1e-8) + 0.1 * ww)).astype(bf)
-            mo[i][0], vo[i][0] = mm, vv
-    def tile(i): return pl.BlockSpec((1, TF, LANES), lambda l, j: ((1 - l) * OFFLAY + MATS * j + i, 0, 0))
-    a, d = pl.BlockSpec((1, LANES, TF), lambda l, j: (l, 0, j)), pl.BlockSpec((1, SUB, D), lambda l, j: (l, j, 0))
+        def out(k, l, i): return cpy(bufs[k][i].at[l], dsts[k][i].at[l], osem.at[k, l, i])
+        for l, i in groups:
+            for k in range(MATS): wt(bufs[k][i].at[l], isem.at[k, l, i])
+            wt(gdb.at[l] if i == TWO else gb.at[l, i], gsem.at[l, i])
+            wb, mb, vb = (bufs[k][i] for k in range(MATS))
+            def one(j):
+                at = (l, blk(j, SUB), slice(None)) if i == TWO else (l, slice(None), blk(j, TF))
+                g = (gdb[at].astype(f32) if i == TWO else gb[l, i, j].astype(f32).T) * factor
+                mm = 0.9 * mb[at] + 0.1 * g
+                vv = 0.95 * vb[at] + 0.05 * g * g
+                ww = wb[at].astype(f32)
+                wb[at] = (ww - 0.02 * (mm * lax.rsqrt(vv + 1e-8) + 0.1 * ww)).astype(bf)
+                mb[at], vb[at] = mm, vv
+            each(0, NT, one)
+            for k in range(MATS): out(k, l, i).start()
+        for l, i in groups:
+            for k in range(MATS): out(k, l, i).wait()
+    hbm = pl.BlockSpec(memory_space=pl.ANY)
+    V, S = pltpu.VMEM, pltpu.SemaphoreType.DMA
     outs = tuple(sds(q.shape, t) for t in (bf, f32, f32) for q in w)
     return pl.pallas_call(
-        kernel, grid=(TWO, NT), in_specs=[pl.BlockSpec((DEV, LANES), lambda l, j: (0, 0)), tile(1), tile(TWO), d] + [a, a, d] * MATS,
-        out_specs=(a, a, d) * MATS, out_shape=outs,
-        compiler_params=pltpu.CompilerParams(vmem_limit_bytes=VMEM_LIMIT, dimension_semantics=("arbitrary",) * TWO),
-        name="optimizer")(sq, GT, GT, GD, *w, *m, *v)
+        kernel, in_specs=[pl.BlockSpec(memory_space=pltpu.VMEM)] + [hbm] * (TWO + MATS * MATS), out_specs=(hbm,) * len(outs), out_shape=outs,
+        scratch_shapes=[V(q.shape, q.dtype) for q in outs] + [V((TWO, TWO, NT, TF, LANES), bf), V((TWO, SH, D), bf), S((MATS, TWO, MATS)), S((MATS, TWO, MATS)), S((TWO, MATS))],
+        compiler_params=pltpu.CompilerParams(vmem_limit_bytes=VMEM_LIMIT),
+        name="optimizer")(sq, GT, GD, *w, *m, *v)
 
 
 def solution(mesh):

time: 363 us -> 357 us (0.983)
  Pallas kernels: 362 us -> 356 us
    pallas_call x1, Pallas kernels: 342 us -> 337 us  [train(): pl.pallas_call(step_kernel, out_shape=outs, in_specs=[hbm] * (MATS + TWO)...]
where the time goes in v4:
time: 357 us
  Pallas kernels  356 us (100%)
    pallas_call x1, Pallas kernels, train(): pl.pallas_call(step_kernel, out_shape=outs, in_specs=[hbm] * (MATS + TWO)...  337 us
    pallas_call x1, Pallas kernels, optimizer(): pl.pallas_call(kernel, in_specs=[pl.BlockSpec(memory_space=pltpu.VMEM)] +...  19.1 us

profile of v4, /device:TPU:1, one launch (start us, length us, event | category | flops | bytes accessed | tf_op | source)
XLA Modules:
  0.0 357.0 jit_solution(13680457850595278752)
XLA Ops:
  0.6 337.0 %train.1 = (bf16[30,640,128]{2,1,0:T(8,128)(2,1)}, bf16[2,400,1024]{2,1,0:T(8,128)(2,1)}, f32[8,128]{1,0:T(8,128)}, bf16[2,8,2,128,3200]{4,3,2,1,0:T(8,128)(2,1)...) custom-call(bf16[2048,1024]{1,0:T(8,128)(2,1)} %bitcast.2, ...), custom_call_target="tpu_custom_call" | custom-call | tf_op jit(solution)/shard_map/train/pallas_call | solution.py:453
  337.7 19.1 %optimizer.1 = (bf16[2,128,3200]{2,1,0:T(8,128)(2,1)}, bf16[2,128,3200]{2,1,0:T(8,128)(2,1)}, bf16[2,400,1024]{2,1,0:T(8,128)(2,1)}, f32[2,128,3200]{2,1,0:T(8,1...) custom-call(f32[8,128]{1,0:T(8,128)} %get-tuple-element.12.sq, ...), custom_call_target="tpu_custom_call" | custom-call | tf_op jit(solution)/shard_map/optimizer/pallas_call | solution.py:499

commit v5 on v4

--- a/solution.py
+++ b/solution.py
@@ -262,8 +262,7 @@
         hr = blk(hs, TF)
         @pl.when(j >= MATS)
         def _(): wt(H.at[cut(TF)], hsem.at[hs])
-        @pl.when(j > 0)
-        def _(): guard(A2, j + 1)
+        guard(A2, j + 1)
         def sub(s):
             @pl.when(j > 0)
             def _(): wt(stv(0), stsem.at[s])
@@ -279,8 +278,6 @@
             cpy(stv(s), AB_h.at[TWO * j + s], stsem.at[s]).start()
             @pl.when(s == 0)
             def _():
-                @pl.when(j == 0)
-                def _(): A2(j + 1)
                 guard(A3, j + 1)
                 @pl.when(j < NT - 1)
                 def _(): gu_load(0, j + 1, 1 - b)
@@ -476,7 +473,6 @@
             else: start([cpy(GT.at[(1 - l) * OFFLAY + MATS * j + i + 1], gb.at[l, i, j], gsem.at[l, i]) for j in range(NT)])
         tot = jnp.sum(jnp.sum(sq[...], axis=0, keepdims=True), axis=1, keepdims=True)
         factor = jnp.minimum(1.0, 0.5 * lax.rsqrt(tot / (TWO * MATS * D * F) + 1e-30))
-        def out(k, l, i): return cpy(bufs[k][i].at[l], dsts[k][i].at[l], osem.at[k, l, i])
         for l, i in groups:
             for k in range(MATS): wt(bufs[k][i].at[l], isem.at[k, l, i])
             wt(gdb.at[l] if i == TWO else gb.at[l, i], gsem.at[l, i])
@@ -489,10 +485,10 @@
                 ww = wb[at].astype(f32)
                 wb[at] = (ww - 0.02 * (mm * lax.rsqrt(vv + 1e-8) + 0.1 * ww)).astype(bf)
                 mb[at], vb[at] = mm, vv
+                for k in range(MATS): cpy(bufs[k][i].at[at], dsts[k][i].at[at], osem.at[k, l, i]).start()
             each(0, NT, one)
-            for k in range(MATS): out(k, l, i).start()
         for l, i in groups:
-            for k in range(MATS): out(k, l, i).wait()
+            for k in range(MATS): wt(bufs[k][i].at[l], osem.at[k, l, i])
     hbm = pl.BlockSpec(memory_space=pl.ANY)
     V, S = pltpu.VMEM, pltpu.SemaphoreType.DMA
     outs = tuple(sds(q.shape, t) for t in (bf, f32, f32) for q in w)

time: 357 us -> 356 us (level)
  no operation moved by 1% of the time
where the time goes in v5:
time: 356 us; the launch traced here: 355 us
  Pallas kernels  355 us (100%)
    pallas_call x1, Pallas kernels, train(): pl.pallas_call(step_kernel, out_shape=outs, in_specs=[hbm] * (MATS + TWO)...  336 us
    pallas_call x1, Pallas kernels, optimizer(): pl.pallas_call(kernel, in_specs=[pl.BlockSpec(memory_space=pltpu.VMEM)] +...  18.5 us

profile of v5, /device:TPU:1, one launch (start us, length us, event | category | flops | bytes accessed | tf_op | source)
XLA Modules:
  0.0 355.5 jit_solution(17634876519058671055)
XLA Ops:
  0.6 336.2 %train.1 = (bf16[30,640,128]{2,1,0:T(8,128)(2,1)}, bf16[2,400,1024]{2,1,0:T(8,128)(2,1)}, f32[8,128]{1,0:T(8,128)}, bf16[2,8,2,128,3200]{4,3,2,1,0:T(8,128)(2,1)...) custom-call(bf16[2048,1024]{1,0:T(8,128)(2,1)} %bitcast.2, ...), custom_call_target="tpu_custom_call" | custom-call | tf_op jit(solution)/shard_map/train/pallas_call | solution.py:450
  336.8 18.5 %optimizer.1 = (bf16[2,128,3200]{2,1,0:T(8,128)(2,1)}, bf16[2,128,3200]{2,1,0:T(8,128)(2,1)}, bf16[2,400,1024]{2,1,0:T(8,128)(2,1)}, f32[2,128,3200]{2,1,0:T(8,1...) custom-call(f32[8,128]{1,0:T(8,128)} %get-tuple-element.12.sq, ...), custom_call_target="tpu_custom_call" | custom-call | tf_op jit(solution)/shard_map/optimizer/pallas_call | solution.py:495
